TPU v7x, 32 devices: a 4x4x1 block of a 4x4x8 slice. The times are simulated.
32 devices in a mesh: dp: 1 (over z), ep_b: 4 (over y), ep_a: 8 (over x, core).
Axes of the slice: x: 4, y: 4, z: 1, core: 2. Of those that a mesh axis runs over, the one named last changes fastest.
The devices are a block of a 4x4x8 slice.
Arguments:
- tokens: bfloat16 [32, 8192, 384], P(('dp', 'ep_b', 'ep_a'))
- expert_ids: int32 [32, 8192], P(('dp', 'ep_b', 'ep_a'))
- route_order: int32 [32, 8192], P(('dp', 'ep_b', 'ep_a'))
- w_route: bfloat16 [384, 256], replicated
- expert_keys: bfloat16 [32, 256], replicated
- temperature: float32 [], replicated
- w_in: bfloat16 [32, 384, 1536], P(('ep_b', 'ep_a'))
- b_in: bfloat16 [32, 1536], P(('ep_b', 'ep_a'))
- w_out: bfloat16 [32, 1536, 384], P(('ep_b', 'ep_a'))
- b_out: bfloat16 [32, 384], P(('ep_b', 'ep_a'))
Outputs:
- output: bfloat16 [32, 8192, 384], P(('dp', 'ep_b', 'ep_a'))
All inputs are finite; a program needn't handle non-finite values.
Results may differ from a plain program's by a relative error of at most 0.00500943.
Values are sent between devices in bfloat16 or wider.
A program may use at most 768 MiB of HBM per device.

v0:
```python
import jax
import jax.numpy as jnp
from jax import lax
from jax.sharding import PartitionSpec as P

EXPERT_AXES = ("ep_b", "ep_a")


def route_local(tok_rows, id_row, order_row, w_route, expert_keys, value_a11, capacity):
    num_experts = expert_keys.shape[0]
    tok_dev = tok_rows.shape[0]
    keys_f32 = expert_keys.astype(jnp.float32)
    key_unit = keys_f32 / jnp.sqrt(jnp.sum(keys_f32 * keys_f32, axis=1, keepdims=True))
    projected = jnp.dot(tok_rows, w_route, preferred_element_type=jnp.float32)
    proj_unit = projected / jnp.sqrt(jnp.sum(projected * projected, axis=1, keepdims=True))
    router_prob = jax.nn.softmax(jnp.dot(proj_unit, key_unit.T) / value_a11, axis=1)
    expert_range = jnp.arange(num_experts, dtype=jnp.int32)[None, :]
    gate_prob = jnp.sum(jnp.where(id_row[:, None] == expert_range, router_prob, 0.0), axis=1)
    ranked_ids = jnp.take(id_row, order_row)
    ranked_hot = (ranked_ids[:, None] == expert_range).astype(jnp.int32)
    ranked_pos = jnp.sum(jnp.cumsum(ranked_hot, axis=0) * ranked_hot, axis=1) - 1
    ranked_slot = jnp.where(ranked_pos < capacity, ranked_ids * capacity + ranked_pos, num_experts * capacity)
    slot_source = jnp.full((num_experts * capacity,), tok_dev, jnp.int32).at[ranked_slot].set(order_row, mode="drop")
    dest_slot = jnp.zeros((tok_dev,), jnp.int32).at[order_row].set(ranked_slot)
    send_rows = jnp.take(tok_rows, slot_source, axis=0, mode="fill", fill_value=0)
    return send_rows, gate_prob, dest_slot


def expert_local(slot_rows, w_first, b_first, w_second, b_second):
    hidden = jnp.dot(slot_rows, w_first, preferred_element_type=jnp.float32) + b_first.astype(jnp.float32)
    hidden = jax.nn.gelu(hidden, approximate=False).astype(jnp.bfloat16)
    result = jnp.dot(hidden, w_second, preferred_element_type=jnp.float32) + b_second.astype(jnp.float32)
    return result.astype(jnp.bfloat16)


def combine_local(back_rows, dest_slot, gate_prob):
    picked = jnp.take(back_rows, dest_slot, axis=0, mode="fill", fill_value=0)
    return (gate_prob[:, None] * picked.astype(jnp.float32)).astype(jnp.bfloat16)


def solution(mesh):
    num_experts = mesh.shape["ep_b"] * mesh.shape["ep_a"]
    tok_spec = P(("dp",) + EXPERT_AXES)
    expert_spec = P(EXPERT_AXES)

    def device_step(tokens, expert_ids, route_order, w_route, expert_keys, value_a11, w_in, b_in, w_out, b_out):
        tok_dev, model_width = tokens.shape[1], tokens.shape[2]
        capacity = (5 * tok_dev + 4 * num_experts - 1) // (4 * num_experts)
        send_rows, gate_prob, dest_slot = route_local(tokens[0], expert_ids[0], route_order[0], w_route, expert_keys, value_a11, capacity)
        arrived = lax.all_to_all(send_rows.reshape(num_experts, capacity, model_width), EXPERT_AXES, 0, 0, tiled=True)
        expert_rows = expert_local(arrived.reshape(num_experts * capacity, model_width), w_in[0], b_in[0], w_out[0], b_out[0])
        returned = lax.all_to_all(expert_rows.reshape(num_experts, capacity, model_width), EXPERT_AXES, 0, 0, tiled=True)
        return combine_local(returned.reshape(num_experts * capacity, model_width), dest_slot, gate_prob)[None]

    return jax.shard_map(
        device_step,
        mesh=mesh,
        in_specs=(tok_spec, tok_spec, tok_spec, P(), P(), P(), expert_spec, expert_spec, expert_spec, expert_spec),
        out_specs=tok_spec,
        check_vma=False,
    )
```

profile of v0, /device:TPU:97, one launch (start us, length us, event | category | flops | bytes accessed | tf_op | source)
XLA Modules:
  0.0 567.9 jit_solution(5523469624592689146)
XLA Ops:
  0.0 0.0 copy-start
  0.0 0.0 copy-start.3
  0.0 0.9 compare_select_fusion.1
  0.9 0.0 copy-start.5
  0.9 0.6 copy-done.5
  1.5 37.4 %gather_fusion = s32[8192]{0:T(1024)S(1)} fusion(s32[8192]{0:T(1024)} %bitcast.57, s32[8192]{0:T(1024)S(1)} %broadcast_clamp_fusion), kind=kCustom, calls=%fused_computation | custom fusion | bytes 98304 | tf_op jit(solution)/shard_map/jit(_take)/gather | solution.py:19
  38.9 0.0 copy-done.3
  38.9 0.1 fusion.45
  39.0 9.5 %reduce-window.6 = s32[32,64,128]{2,1,0:T(8,128)S(1)} reduce-window(s32[32,64,128]{2,1,0:T(8,128)S(1)} %fusion.45, s32[]{:T(128)} %constant.42.clone.1), window={size=1x1x128 pad=0_0x0_0x127_0}, to_apply=%region_5.6 | reduce-window | flops 33292288 | bytes 2097156 | tf_op jit(solution)/shard_map/reduce-window
  48.6 0.9 slice_reduce_fusion
  49.5 0.2 reduce-window.9
  49.7 0.3 broadcast_add_fusion
  50.1 0.8 fusion.44
  50.8 0.6 add_select_fusion
  51.5 0.1 compare_select_fusion
  51.6 30.5 %scatter_custom_fusion.1 = s32[10240]{0:T(1024)S(1)} fusion(s32[8192]{0:T(1024)S(1)} %bitcast.71, s32[8192]{0:T(1024)S(1)} %bitcast.65, s32[]{:T(128)} %constant.43.clone.1), kind=kCustom, calls=%fused_computation.91 | custom fusion | bytes 40964 | tf_op jit(solution)/shard_map/scatter | solution.py:23
  82.1 0.1 broadcast_in_dim.69
  82.2 43.9 %gather_fusion.1 = bf16[10240,384]{1,0:T(8,128)(2,1)} fusion(bf16[8192,384]{1,0:T(8,128)(2,1)} %bitcast.59, s32[10240]{0:T(1024)S(1)} %fusion.47), kind=kCustom, calls=%fused_computation.1 | custom fusion | bytes 15769600 | tf_op jit(solution)/shard_map/jit(_take)/gather | solution.py:25
  126.1 0.0 copy-start.9
  126.1 0.0 copy-start.7
  126.1 7.3 %broadcast_select_fusion = bf16[32,320,384]{2,1,0:T(8,128)(2,1)} fusion(bf16[32,320,384]{2,1,0:T(8,128)(2,1)} %bitcast.60, pred[32,320]{1,0:T(8,128)(4,1)S(1)} %broadcast_in_dim.69), kind=kLoop, calls=%fused_computation.56 | loop fusion | flops 3932160 | bytes 15738880 | tf_op jit(solution)/shard_map/jit(_take)/select_n | solution.py:25
  133.4 9.2 %all-to-all-start = ((bf16[32,320,384]{2,1,0:T(8,128)(2,1)}), bf16[32,320,384]{2,1,0:T(8,128)(2,1)}, u32[]{:S(2)}, u32[]{:S(2)}) async-start(bf16[32,320,384]{2,1,0:T(8,128)(2,1)} %broadcast_select_fusion), calls=%async_computation | async-start | bytes 15728640 | tf_op jit(solution)/shard_map/all_to_all | solution.py:50
  142.6 0.0 copy-done.9
  142.6 0.6 convert_reduce_fusion.1
  143.2 0.0 copy-done.7
  143.2 95.5 %all-to-all-done = bf16[32,320,384]{2,1,0:T(8,128)(2,1)} async-done(((bf16[32,320,384]{2,1,0:T(8,128)(2,1)}), bf16[32,320,384]{2,1,0:T(8,128)(2,1)}, u32[]{:S(2)}, u32[]{:S(2)}) %all-to-all-start) | async-done | bytes 7864352 | tf_op jit(solution)/shard_map/all_to_all | solution.py:50
  238.7 0.0 copy-done
  238.7 0.0 copy-start.8
  238.7 0.0 copy-start.10
  238.7 148.6 %fusion.2.clone.8 = bf16[10240,1536]{1,0:T(8,128)(2,1)} fusion(bf16[10240,384]{1,0:T(8,128)(2,1)} %bitcast.12, f32[1536]{0:T(1024)S(1)} %convert_reduce_fusion, bf16[1,384,1536]{2,1,0:T(8,128)(2,1)S(1)} %copy-done), kind=kOutput, calls=%fused_computation.8.clone.clone.clone.clone.clone.clone.clone.1 | convolution fusion | flops 13117685760 | bytes 40507392 | tf_op jit(solution)/shard_map/dot_general | solution.py:30
  387.3 0.0 copy-done.8
  387.3 0.0 copy-done.10
  387.3 0.0 copy-start.4
  387.4 22.5 %fusion.37 = bf16[10240,384]{1,0:T(8,128)(2,1)} fusion(f32[384]{0:T(512)S(1)} %copy-done.8, bf16[1,1536,384]{2,1,0:T(8,128)(2,1)S(1)} %copy-done.10, bf16[10240,1536]{1,0:T(8,128)(2,1)} %fusion.2.clone.8), kind=kOutput, calls=%fused_computation.51 | convolution fusion | flops 12087459840 | bytes 40502784 | tf_op jit(solution)/shard_map/dot_general | solution.py:32
  409.9 13.3 %all-to-all-start.1 = ((bf16[32,320,384]{2,1,0:T(8,128)(2,1)}), bf16[32,320,384]{2,1,0:T(8,128)(2,1)}, u32[]{:S(2)}, u32[]{:S(2)}) async-start(bf16[32,320,384]{2,1,0:T(8,128)(2,1)} %bitcast.61), calls=%async_computation.1 | async-start | bytes 15728640 | tf_op jit(solution)/shard_map/all_to_all | solution.py:52
  423.2 30.8 %scatter_custom_fusion = s32[8192]{0:T(1024)S(1)} fusion(s32[8192]{0:T(1024)} %bitcast.68, s32[8192]{0:T(1024)} %get-tuple-element.5, s32[]{:T(128)} %constant.42.clone.1), kind=kCustom, calls=%fused_computation.95 | custom fusion | bytes 33280 | tf_op jit(solution)/shard_map/scatter | solution.py:24
  454.0 0.0 copy-done.4
  454.1 8.4 %multiply_reduce_fusion = (f32[8192]{0:T(1024)S(1)}, f32[8192,256]{0,1:T(8,128)}) fusion(bf16[384,256]{1,0:T(8,128)(2,1)S(1)} %copy-done.4, bf16[1,8192,384]{2,1,0:T(8,128)(2,1)} %param.10), kind=kOutput, calls=%fused_computation.54 | convolution fusion | flops 1614798848 | bytes 14909440 | tf_op jit(solution)/shard_map/dot_general | solution.py:14
  462.5 0.0 copy-done.6
  462.5 0.1 fusion.48
  463.3 4.4 fusion.87
  467.7 0.2 fusion.46
  467.9 0.0 copy-done.2
  468.0 0.3 select_reduce_fusion
  468.3 53.7 %all-to-all-done.1 = bf16[32,320,384]{2,1,0:T(8,128)(2,1)} async-done(((bf16[32,320,384]{2,1,0:T(8,128)(2,1)}), bf16[32,320,384]{2,1,0:T(8,128)(2,1)}, u32[]{:S(2)}, u32[]{:S(2)}) %all-to-all-start.1) | async-done | bytes 7864352 | tf_op jit(solution)/shard_map/all_to_all | solution.py:52
  521.9 36.9 %gather_fusion.2 = bf16[8192,384]{1,0:T(8,128)(2,1)} fusion(bf16[10240,384]{1,0:T(8,128)(2,1)} %bitcast.16, s32[8192]{0:T(1024)S(1)} %fusion.49), kind=kCustom, calls=%fused_computation.2 | custom fusion | bytes 12615680 | tf_op jit(solution)/shard_map/jit(_take)/gather | solution.py:37
  558.8 9.1 %multiply_convert_fusion = bf16[1,8192,384]{2,1,0:T(8,128)(2,1)} fusion(bf16[8192,384]{1,0:T(8,128)(2,1)} %gather_fusion.2, f32[8192]{0:T(1024)S(1)} %select_reduce_fusion, pred[8192]{0:T(1024)(128)(4,1)S(1)} %compare_and_fusion.1), kind=kLoop, calls=%fused_computation.52 | loop fusion | flops 12582912 | bytes 12623872 | tf_op jit(solution)/shard_map/convert_element_type | solution.py:38
  567.9 0.0 copy-done.1
  (13 shorter events, 0.1 us)
Async XLA Ops:
  0.0 238.7 %copy-start = (bf16[1,384,1536]{2,1,0:T(8,128)(2,1)S(1)}, bf16[1,384,1536]{2,1,0:T(8,128)(2,1)}, u32[]{:S(2)}) copy-start(bf16[1,384,1536]{2,1,0:T(8,128)(2,1)} %param.16) | copy-start | bytes 3538948
  0.0 38.9 %copy-start.3 = (s32[1,8192]{1,0:T(1,128)S(1)}, s32[1,8192]{1,0:T(1,128)}, u32[]{:S(2)}) copy-start(s32[1,8192]{1,0:T(1,128)} %param.12) | copy-start | bytes 98308
  0.9 0.6 copy-start.5
  126.1 16.5 %copy-start.9 = (bf16[1,384]{1,0:T(2,128)(2,1)S(1)}, bf16[1,384]{1,0:T(2,128)(2,1)}, u32[]{:S(2)}) copy-start(bf16[1,384]{1,0:T(2,128)(2,1)} %param.19) | copy-start | bytes 2308
  126.1 17.1 %copy-start.7 = (bf16[1,1536]{1,0:T(2,128)(2,1)S(1)}, bf16[1,1536]{1,0:T(2,128)(2,1)}, u32[]{:S(2)}) copy-start(bf16[1,1536]{1,0:T(2,128)(2,1)} %param.17) | copy-start | bytes 9220
  133.4 105.3 %all-to-all-start = ((bf16[32,320,384]{2,1,0:T(8,128)(2,1)}), bf16[32,320,384]{2,1,0:T(8,128)(2,1)}, u32[]{:S(2)}, u32[]{:S(2)}) async-start(bf16[32,320,384]{2,1,0:T(8,128)(2,1)} %broadcast_select_fusion), calls=%async_computation | async-start | bytes 15728640 | tf_op jit(solution)/shard_map/all_to_all | solution.py:50
  238.7 148.6 %copy-start.8 = (f32[384]{0:T(512)S(1)}, f32[384]{0:T(512)}, u32[]{:S(2)}) copy-start(f32[384]{0:T(512)} %convert_reduce_fusion.1) | copy-start | bytes 4612
  238.7 148.6 %copy-start.10 = (bf16[1,1536,384]{2,1,0:T(8,128)(2,1)S(1)}, bf16[1,1536,384]{2,1,0:T(8,128)(2,1)}, u32[]{:S(2)}) copy-start(bf16[1,1536,384]{2,1,0:T(8,128)(2,1)} %param.18) | copy-start | bytes 3538948
  387.3 66.7 %copy-start.4 = (bf16[384,256]{1,0:T(8,128)(2,1)S(1)}, bf16[384,256]{1,0:T(8,128)(2,1)}, u32[]{:S(2)}) copy-start(bf16[384,256]{1,0:T(8,128)(2,1)} %param.13) | copy-start | bytes 589828
  409.9 52.6 %copy-start.6 = (bf16[32,256]{1,0:T(8,128)(2,1)S(1)}, bf16[32,256]{1,0:T(8,128)(2,1)}, u32[]{:S(2)}) copy-start(bf16[32,256]{1,0:T(8,128)(2,1)} %param.14) | copy-start | bytes 49156
  409.9 58.1 %copy-start.2 = (s32[1,8192]{1,0:T(1,128)S(1)}, s32[1,8192]{1,0:T(1,128)}, u32[]{:S(2)}) copy-start(s32[1,8192]{1,0:T(1,128)} %param.11) | copy-start | bytes 98308
  409.9 112.1 %all-to-all-start.1 = ((bf16[32,320,384]{2,1,0:T(8,128)(2,1)}), bf16[32,320,384]{2,1,0:T(8,128)(2,1)}, u32[]{:S(2)}, u32[]{:S(2)}) async-start(bf16[32,320,384]{2,1,0:T(8,128)(2,1)} %bitcast.61), calls=%async_computation.1 | async-start | bytes 15728640 | tf_op jit(solution)/shard_map/all_to_all | solution.py:52
  521.9 46.0 %copy-start.1 = (bf16[1,384,1536]{2,1,0:T(8,128)(2,1)S(1)}, bf16[1,384,1536]{2,1,0:T(8,128)(2,1)}, u32[]{:S(2)}) copy-start(bf16[1,384,1536]{2,1,0:T(8,128)(2,1)} %param.16) | copy-start | bytes 3538948
where the time goes:
time: 575 us; the launch traced here: 568 us
  matrix products  184 us (32%)
  local copies, waits for them, and re-layouts  181 us (31%)
  waiting for transfers between devices  149 us (26%)
  other arithmetic  30.3 us (5%)
  starting transfers between devices  22.5 us (4%)
    dot_general x1, matrix products, expert_local(): jnp.dot(slot_rows, w_first, preferred_element_type=jnp.float32)  149 us
    all_to_all x1, waiting for transfers between devices, device_step(): lax.all_to_all(send_rows.reshape(num_experts, capacity, model_width), EXP...  95.5 us
    all_to_all x1, waiting for transfers between devices, device_step(): lax.all_to_all(expert_rows.reshape(num_experts, capacity, model_width), E...  53.7 us
    gather x1, local copies, waits for them, and re-layouts, route_local(): jnp.take(tok_rows, slot_source, axis=0, mode='fill', fill_value=0)  43.9 us
    gather x1, local copies, waits for them, and re-layouts, route_local(): ranked_ids = jnp.take(id_row, order_row)  37.4 us
    gather x1, local copies, waits for them, and re-layouts, combine_local(): picked = jnp.take(back_rows, dest_slot, axis=0, mode='fill', fill_value=0)  36.9 us
    scatter x1, local copies, waits for them, and re-layouts, route_local(): dest_slot = jnp.zeros((tok_dev,), jnp.int32).at[order_row].set(ranked_slot)  30.8 us
    scatter x1, local copies, waits for them, and re-layouts, route_local(): jnp.full((num_experts * capacity,), tok_dev, jnp.int32).at[ranked_slot]  30.5 us
  transfers between devices with their start and end apart: 2, of which 2 were waited for; matrix products, arithmetic and copies ran while one was open for 8% of the time, Pallas kernels for 0%

commit v1 on v0

v1 whole, which is shorter than its diff:
```python
import functools

import jax
import jax.numpy as jnp
from jax import lax
from jax.experimental import pallas as pl
from jax.experimental.pallas import tpu as pltpu
from jax.sharding import PartitionSpec as P

EXPERT_AXES = ("ep_b", "ep_a")
LANES = 128
MESH_ID = pl.DeviceIdType.MESH
F32 = jnp.float32
BF16 = jnp.bfloat16


def iota(shape, dim):
    return lax.broadcasted_iota(jnp.int32, shape, dim)


def dot_nt(a, b):
    return lax.dot_general(a, b, (((1,), (1,)), ((), ())), preferred_element_type=F32)


def as_bf16(mask):
    return jnp.where(mask, 1.0, 0.0).astype(BF16)


def virtual_expert(ids, size_b, size_x):
    i_b, i_a = ids // (2 * size_x), ids % (2 * size_x)
    x, core = i_a // 2, i_a % 2
    return jnp.where(core == 0, x * size_b + i_b, size_b * size_x + i_b * size_x + x)


def dispatch_kernel(dims, ids_ref, order_ref, tok_hbm, send_hbm, dest_ref,
                    tok_vm, big, src_vm, src_sm, tmp, out_vm, tok_sem, src_sem, out_sem):
    size_b, size_x, cap = dims
    rows = ids_ref.shape[0]
    num_experts = 2 * size_b * size_x
    width = tok_vm.shape[1]
    parts = width // LANES
    slot_rows = src_vm.shape[0]
    tok_copy = pltpu.make_async_copy(tok_hbm, tok_vm, tok_sem)
    tok_copy.start()

    upper = as_bf16((iota((LANES, 2 * LANES), 0) <= iota((LANES, 2 * LANES), 1)) | (iota((LANES, 2 * LANES), 1) >= LANES))
    ids_t = ids_ref[...].astype(F32).T.astype(BF16)
    iota_rows = iota((rows, LANES), 0)
    iota_lane = iota((LANES, LANES), 0)
    iota_exp = iota((num_experts, LANES), 0)

    def ranked(r, carry):
        count, keep = carry
        o = order_ref[pl.ds(r, 1), :]
        hi, lo = o // LANES, o % LANES
        pick_hi = iota_rows == hi
        pick_lo = iota_lane == lo
        table = jnp.dot(ids_t, as_bf16(pick_hi), preferred_element_type=F32)
        rid = jnp.sum(jnp.where(pick_lo, table, 0.0), axis=0, keepdims=True)
        mine = iota_exp.astype(F32) == rid
        both = jnp.dot(as_bf16(mine), upper, preferred_element_type=F32)
        rank = jnp.sum(jnp.where(mine, both[:, :LANES] + count, 0.0), axis=0, keepdims=True)
        kept = rank <= float(cap)
        keep = keep + dot_nt(as_bf16(pick_hi & kept), as_bf16(pick_lo))
        return count + both[:, LANES:], keep

    zero_count = jnp.zeros((num_experts, LANES), F32)
    _, keep = lax.fori_loop(0, rows, ranked, (zero_count, jnp.zeros((rows, LANES), F32)), unroll=8)
    dest_ref[...] = keep.astype(jnp.int32)

    iota_slot = iota((slot_rows, LANES), 0)
    lane = iota((1, LANES), 1).astype(F32)

    def placed(r, carry):
        count, source = carry
        expert = virtual_expert(ids_ref[pl.ds(r, 1), :], size_b, size_x)
        kept = dest_ref[pl.ds(r, 1), :] > 0
        mine = (iota_exp == expert) & kept
        both = jnp.dot(as_bf16(mine), upper, preferred_element_type=F32)
        pos = jnp.sum(jnp.where(mine, both[:, :LANES] + count, 0.0), axis=0, keepdims=True) - 1.0
        slot = jnp.where(kept, expert * cap + pos.astype(jnp.int32), num_experts * cap)
        dest_ref[pl.ds(r, 1), :] = slot * parts
        pick = jnp.where(iota_slot == slot // LANES, 1.0, 0.0)
        stacked = jnp.concatenate([pick * lax.convert_element_type(r, F32), pick * lane], axis=0).astype(BF16)
        source = source + dot_nt(stacked, as_bf16(iota_lane == slot % LANES))
        return count + both[:, LANES:], source

    _, source = lax.fori_loop(0, rows, placed, (zero_count, jnp.zeros((2 * slot_rows, LANES), F32)), unroll=4)
    src_vm[...] = ((source[:slot_rows] * float(LANES) + source[slot_rows:]) * float(parts)).astype(jnp.int32)
    src_copy = pltpu.make_async_copy(src_vm, src_sm, src_sem)
    src_copy.start()

    tok_copy.wait()

    def widen(i, _):
        base = pl.multiple_of(i * 16, 16)
        for c in range(parts):
            big[pl.ds(base * parts + c, 16, stride=parts), :] = tok_vm[pl.ds(base, 16), c * LANES:(c + 1) * LANES].astype(F32)
        return 0

    lax.fori_loop(0, tok_vm.shape[0] // 16, widen, 0, unroll=8)
    src_copy.wait()

    def out_copy(i):
        return pltpu.make_async_copy(out_vm.at[lax.rem(i, 4)], send_hbm.at[pl.ds(pl.multiple_of(i * LANES, LANES), LANES)],
                                     out_sem.at[lax.rem(i, 4)])

    def gather(i, _):
        @pl.when(i >= 4)
        def _():
            out_copy(i - 4).wait()
        slot = lax.rem(i, 4)
        for j in range(LANES):
            tmp[pl.ds(j * parts, parts), :] = big[pl.ds(src_sm[i, j], parts), :]
        for j in range(0, LANES, 16):
            for c in range(parts):
                out_vm[slot, pl.ds(j, 16), c * LANES:(c + 1) * LANES] = tmp[pl.ds(j * parts + c, 16, stride=parts), :].astype(BF16)
        out_copy(i).start()
        return 0

    lax.fori_loop(0, slot_rows, gather, 0)
    for i in range(slot_rows - 4, slot_rows):
        out_copy(i).wait()


def dispatch(tok_rows, ids, order, dims):
    size_b, size_x, cap = dims
    tok_dev, width = tok_rows.shape
    slots = 2 * size_b * size_x * cap
    rows, slot_rows, parts = tok_dev // LANES, slots // LANES, width // LANES
    vmem, hbm = pl.BlockSpec(memory_space=pltpu.VMEM), pl.BlockSpec(memory_space=pltpu.HBM)
    return pl.pallas_call(
        functools.partial(dispatch_kernel, dims),
        name="dispatch",
        out_shape=(jax.ShapeDtypeStruct((slots, width), BF16), jax.ShapeDtypeStruct((rows, LANES), jnp.int32)),
        in_specs=[vmem, vmem, hbm],
        out_specs=(hbm, vmem),
        scratch_shapes=[
            pltpu.VMEM((tok_dev, width), BF16),
            pltpu.VMEM((tok_dev * parts, LANES), F32),
            pltpu.VMEM((slot_rows, LANES), jnp.int32),
            pltpu.SMEM((slot_rows, LANES), jnp.int32),
            pltpu.VMEM((LANES * parts, LANES), F32),
            pltpu.VMEM((4, LANES, width), BF16),
            pltpu.SemaphoreType.DMA,
            pltpu.SemaphoreType.DMA,
            pltpu.SemaphoreType.DMA((4,)),
        ],
        compiler_params=pltpu.CompilerParams(vmem_limit_bytes=40 << 20),
        cost_estimate=pl.CostEstimate(flops=20_000_000_000, bytes_accessed=15_000_000, transcendentals=0),
    )(ids.reshape(rows, LANES), order.reshape(rows, LANES), tok_rows)


def peers(dims, pos_x, pos_y, core):
    size_b, size_x, _ = dims

    def sends_to(kind, k):
        return (pos_y, 2 * k) if kind == 0 else (k, 2 * pos_x + 1)

    def serves(k, c):
        return (core * k + (1 - core) * pos_y, 2 * (core * pos_x + (1 - core) * k) + c)

    return sends_to, serves


def exchange_kernel(dims, send_hbm, *refs):
    size_b, size_x, cap = dims
    n = size_x
    w1_hbm, w2_hbm = refs[:n], refs[n:2 * n]
    b1_ref, b2_ref, back_hbm, w1, w2, recv, result, w_sem, out_sem, in_sem, ret_sem, back_sem = refs[2 * n:]
    i_b, i_a = lax.axis_index("ep_b"), lax.axis_index("ep_a")
    i_dp = lax.axis_index("dp")
    pos_x, core, pos_y = i_a // 2, lax.rem(i_a, 2), i_b
    pos = (1 - core) * pos_x + core * pos_y
    wpos = (1 - core) * pos_y + core * pos_x
    sends_to, serves = peers(dims, pos_x, pos_y, core)

    w_copies = []
    for d in range(n):
        w_copies.append(pltpu.make_async_copy(w1_hbm[d], w1.at[pl.ds(d, 1)], w_sem.at[0, d]))
        w_copies.append(pltpu.make_async_copy(w2_hbm[d], w2.at[pl.ds(d, 1)], w_sem.at[1, d]))
    for copy in w_copies:
        copy.start()

    barrier = pltpu.get_barrier_semaphore()
    for k in range(n):
        for c in range(2):
            for b, a in (sends_to(c, k), serves(k, c)):
                pl.semaphore_signal(barrier, inc=1, device_id=(i_dp, b, a), device_id_type=MESH_ID)
    pl.semaphore_wait(barrier, 4 * n)

    def out_copy(kind, step, j):
        my_place = pos_x if kind == 0 else pos_y
        k = lax.rem(my_place + step, n)
        b, a = sends_to(kind, k)
        src = (kind * n + k) * n + j
        dst = (my_place * n + j) * 2 + core
        return pltpu.make_async_remote_copy(
            src_ref=send_hbm.at[pl.ds(pl.multiple_of(src * cap, cap), cap)],
            dst_ref=recv.at[pl.ds(pl.multiple_of(dst * cap, cap), cap)],
            send_sem=out_sem.at[(kind * n + step) * n + j],
            recv_sem=in_sem.at[dst],
            device_id=(i_dp, b, a), device_id_type=MESH_ID)

    def ret_copy(k, j, c):
        b, a = serves(k, c)
        src = (k * n + j) * 2 + c
        dst = (core * n + pos) * n + j
        return pltpu.make_async_remote_copy(
            src_ref=result.at[pl.ds(pl.multiple_of(src * cap, cap), cap)],
            dst_ref=back_hbm.at[pl.ds(pl.multiple_of(dst * cap, cap), cap)],
            send_sem=ret_sem.at[src],
            recv_sem=back_sem.at[dst],
            device_id=(i_dp, b, a), device_id_type=MESH_ID)

    def send_slots(kind, step, j):
        if step:
            out_copy(kind, step, j).start()
            return

        @pl.when(kind != core)
        def _():
            out_copy(kind, step, j).start()

        @pl.when(kind == core)
        def _():
            own_slots(j).start()

    def own_slots(j):
        src, dst = (core * n + pos) * n + j, (pos * n + j) * 2 + core
        return pltpu.make_async_copy(send_hbm.at[pl.ds(pl.multiple_of(src * cap, cap), cap)],
                                     recv.at[pl.ds(pl.multiple_of(dst * cap, cap), cap)], in_sem.at[dst])

    def own_results(j):
        src, dst = (pos * n + j) * 2 + core, (core * n + pos) * n + j
        return pltpu.make_async_copy(result.at[pl.ds(pl.multiple_of(src * cap, cap), cap)],
                                     back_hbm.at[pl.ds(pl.multiple_of(dst * cap, cap), cap)], back_sem.at[dst])

    steps = [0, 1, n - 1] + list(range(2, n - 1))
    for group in ([0], [1, n - 1], list(range(2, n - 1))):
        for j in range(n):
            for step in group:
                for kind in range(2):
                    send_slots(kind, step, j)

    for copy in w_copies:
        copy.wait()

    def place(t):
        order = jnp.int32(0)
        for i, step in enumerate(steps):
            order = order + jnp.where(t // n == i, step, 0)
        k = lax.rem(pos - order + n, n)
        off = lax.rem(t, n)
        return k, off, lax.rem(wpos + off, n)

    def send_results(t):
        k, _, j = place(t)
        for c in range(2):
            mine = (k == pos) & (core == c)

            @pl.when(mine)
            def _():
                own_results(j).start()

            @pl.when(jnp.logical_not(mine))
            def _(c=c):
                ret_copy(k, j, c).start()

    def serve(t, _):
        k, off, j = place(t)
        first = (k * n + j) * 2
        for c in range(2):
            pltpu.make_async_remote_copy(
                src_ref=send_hbm.at[pl.ds(0, cap)],
                dst_ref=recv.at[pl.ds(pl.multiple_of((first + c) * cap, cap), cap)],
                send_sem=out_sem.at[0], recv_sem=in_sem.at[first + c],
                device_id=(i_dp, i_b, i_a), device_id_type=MESH_ID).wait_recv()
        rows = pl.ds(pl.multiple_of(first * cap, 2 * cap), 2 * cap)
        x = recv[rows, :]
        hidden = jnp.dot(x, w1[off], preferred_element_type=F32) + b1_ref[off].astype(F32)
        hidden = (0.5 * hidden * (1.0 + lax.erf(hidden * (0.5 ** 0.5)))).astype(BF16)
        y = jnp.dot(hidden, w2[off], preferred_element_type=F32) + b2_ref[off].astype(F32)
        result[rows, :] = y.astype(BF16)

        @pl.when(t > 0)
        def _():
            send_results(t - 1)
        return 0

    blocks = n * n
    lax.fori_loop(0, blocks, serve, 0)
    send_results(jnp.int32(blocks - 1))

    def drain(t, _):
        block = pl.ds(pl.multiple_of(t * cap, cap), cap)
        kind, step = t // (n * n), lax.rem(t // n, n)
        sent = pltpu.make_async_remote_copy(
            src_ref=send_hbm.at[block], dst_ref=recv.at[block],
            send_sem=out_sem.at[t], recv_sem=in_sem.at[t],
            device_id=(i_dp, i_b, i_a), device_id_type=MESH_ID)
        returned = pltpu.make_async_remote_copy(
            src_ref=result.at[block], dst_ref=back_hbm.at[block],
            send_sem=ret_sem.at[t], recv_sem=back_sem.at[t],
            device_id=(i_dp, i_b, i_a), device_id_type=MESH_ID)

        @pl.when((kind != core) | (step != 0))
        def _():
            sent.wait_send()

        @pl.when((t // (2 * n) != pos) | (lax.rem(t, 2) != core))
        def _():
            returned.wait_send()

        returned.wait_recv()
        return 0

    lax.fori_loop(0, 2 * blocks, drain, 0)


def exchange(send_rows, w1, b1, w2, b2, dims):
    size_b, size_x, cap = dims
    n = size_x
    slots, width = send_rows.shape
    hidden = w1[0].shape[2]
    vmem, hbm = pl.BlockSpec(memory_space=pltpu.VMEM), pl.BlockSpec(memory_space=pltpu.HBM)
    return pl.pallas_call(
        functools.partial(exchange_kernel, dims),
        name="exchange",
        out_shape=jax.ShapeDtypeStruct((slots, width), BF16),
        in_specs=[pl.BlockSpec(memory_space=pl.ANY)] + [hbm] * (2 * n) + [vmem] * 2,
        out_specs=hbm,
        scratch_shapes=[
            pltpu.VMEM((n, width, hidden), BF16),
            pltpu.VMEM((n, hidden, width), BF16),
            pltpu.VMEM((slots, width), BF16),
            pltpu.VMEM((slots, width), BF16),
            pltpu.SemaphoreType.DMA((2, n)),
            pltpu.SemaphoreType.DMA((2 * n * n,)),
            pltpu.SemaphoreType.DMA((2 * n * n,)),
            pltpu.SemaphoreType.DMA((2 * n * n,)),
            pltpu.SemaphoreType.DMA((2 * n * n,)),
        ],
        compiler_params=pltpu.CompilerParams(collective_id=1, has_side_effects=True, vmem_limit_bytes=60 << 20),
        cost_estimate=pl.CostEstimate(flops=4 * slots * width * hidden, bytes_accessed=30_000_000, transcendentals=0),
    )(send_rows, *w1, *w2, b1, b2)


def combine_kernel(back_hbm, dest_sm, gate_sm, out_ref, stage, big, tmp, sem):
    i = pl.program_id(0)
    slots, width = back_hbm.shape
    parts = width // LANES
    chunk = stage.shape[1]
    chunks = slots // chunk

    @pl.when(i == 0)
    def _():
        def fetch(q):
            return pltpu.make_async_copy(back_hbm.at[pl.ds(pl.multiple_of(q * chunk, chunk), chunk)], stage.at[lax.rem(q, 2)],
                                         sem.at[lax.rem(q, 2)])
        fetch(0).start()
        big[pl.ds(slots * parts, 8), :] = jnp.zeros((8, LANES), F32)

        def widen_chunk(q, _):
            @pl.when(q + 1 < chunks)
            def _():
                fetch(q + 1).start()
            fetch(q).wait()

            def widen(u, _):
                base = pl.multiple_of(u * 16, 16)
                for c in range(parts):
                    big[pl.ds((q * chunk + base) * parts + c, 16, stride=parts), :] = (
                        stage[lax.rem(q, 2), pl.ds(base, 16), c * LANES:(c + 1) * LANES].astype(F32))
                return 0

            lax.fori_loop(0, chunk // 16, widen, 0, unroll=8)
            return 0

        lax.fori_loop(0, chunks, widen_chunk, 0)

    def gather(g, _):
        row = i * (out_ref.shape[0] // LANES) + g
        for j in range(LANES):
            tmp[pl.ds(j * parts, parts), :] = big[pl.ds(dest_sm[row, j], parts), :] * gate_sm[row, j]
        for j in range(0, LANES, 16):
            for c in range(parts):
                out_ref[pl.ds(pl.multiple_of(g * LANES + j, 16), 16), c * LANES:(c + 1) * LANES] = (
                    tmp[pl.ds(j * parts + c, 16, stride=parts), :].astype(BF16))
        return 0

    lax.fori_loop(0, out_ref.shape[0] // LANES, gather, 0)


def combine(back_rows, dest, gate, tok_dev):
    slots, width = back_rows.shape
    parts = width // LANES
    block = 1024
    smem = pl.BlockSpec(memory_space=pltpu.SMEM)
    return pl.pallas_call(
        combine_kernel,
        name="combine",
        grid=(tok_dev // block,),
        out_shape=jax.ShapeDtypeStruct((tok_dev, width), BF16),
        in_specs=[pl.BlockSpec(memory_space=pltpu.HBM), smem, smem],
        out_specs=pl.BlockSpec((block, width), lambda i: (i, 0)),
        scratch_shapes=[
            pltpu.VMEM((2, 1280, width), BF16),
            pltpu.VMEM((slots * parts + 8, LANES), F32),
            pltpu.VMEM((LANES * parts, LANES), F32),
            pltpu.SemaphoreType.DMA((2,)),
        ],
        compiler_params=pltpu.CompilerParams(vmem_limit_bytes=40 << 20, dimension_semantics=("arbitrary",)),
        cost_estimate=pl.CostEstimate(flops=20_000_000_000, bytes_accessed=15_000_000, transcendentals=0),
    )(back_rows, dest, gate)


def gates(tok_rows, id_row, w_route, expert_keys, temperature):
    num_experts = expert_keys.shape[0]
    keys_f32 = expert_keys.astype(F32)
    key_unit = keys_f32 / jnp.sqrt(jnp.sum(keys_f32 * keys_f32, axis=1, keepdims=True))
    projected = jnp.dot(tok_rows, w_route, preferred_element_type=F32)
    proj_unit = projected / jnp.sqrt(jnp.sum(projected * projected, axis=1, keepdims=True))
    router_prob = jax.nn.softmax(jnp.dot(proj_unit, key_unit.T) / temperature, axis=1)
    expert_range = jnp.arange(num_experts, dtype=jnp.int32)[None, :]
    return jnp.sum(jnp.where(id_row[:, None] == expert_range, router_prob, 0.0), axis=1)


def solution(mesh):
    size_b, size_x = mesh.shape["ep_b"], mesh.shape["ep_a"] // 2
    num_experts = 2 * size_b * size_x
    tok_spec = P(("dp",) + EXPERT_AXES)
    expert_spec = P(EXPERT_AXES)

    def share(w):
        out = [w]
        for d in range(1, size_x):
            pairs = []
            for y in range(size_b):
                for x in range(size_x):
                    pairs.append(((y * size_x + x) * 2, (((y - d) % size_b) * size_x + x) * 2))
                    pairs.append(((y * size_x + x) * 2 + 1, (y * size_x + (x - d) % size_x) * 2 + 1))
            out.append(lax.ppermute(w, EXPERT_AXES, pairs))
        return out

    def device_step(tokens, expert_ids, route_order, w_route, expert_keys, temperature, w_in, b_in, w_out, b_out):
        tok_dev = tokens.shape[1]
        cap = (5 * tok_dev + 4 * num_experts - 1) // (4 * num_experts)
        dims = (size_b, size_x, cap)
        w1, w2 = share(w_in), share(w_out)
        b1, b2 = (jnp.concatenate(share(b[:, None, :]), axis=0) for b in (b_in, b_out))
        send_rows, dest = dispatch(tokens[0], expert_ids[0], route_order[0], dims)
        gate = gates(tokens[0], expert_ids[0], w_route, expert_keys, temperature).reshape(tok_dev // LANES, LANES)
        back_rows = exchange(send_rows, w1, b1, w2, b2, dims)
        return combine(back_rows, dest, gate, tok_dev)[None]

    return jax.shard_map(
        device_step,
        mesh=mesh,
        in_specs=(tok_spec, tok_spec, tok_spec, P(), P(), P(), expert_spec, expert_spec, expert_spec, expert_spec),
        out_specs=tok_spec,
        check_vma=False,
    )
```

time: 575 us -> 246 us (0.43)
  matrix products: 184 us -> 10.1 us
  local copies, waits for them, and re-layouts: 181 us -> 8.89 us
  Pallas kernels: 0 us -> 159 us
  waiting for transfers between devices: 149 us -> 43.4 us
  other arithmetic: 30.3 us -> 1.88 us
    dot_general x4 -> x2, matrix products: 184 us -> 10.1 us  [the longest x1 5.71 us: gates(): projected = jnp.dot(tok_rows, w_route, preferred_element_type=F32)]
    pallas_call x0 -> x3, Pallas kernels: none -> 159 us  [the longest x1 97.5 us: exchange(): pl.pallas_call(functools.partial(exchange_kernel, dims), name='exchange',...]
    all_to_all x2 -> x0, waiting for transfers between devices: 149 us -> none  [the longest x1 95.5 us: device_step(): lax.all_to_all(send_rows.reshape(num_experts, capacity, model_width), EXP...]
    gather x3 -> x0, local copies, waits for them, and re-layouts: 118 us -> none  [the longest x1 43.9 us: route_local(): jnp.take(tok_rows, slot_source, axis=0, mode='fill', fill_value=0)]
    scatter x2 -> x0, local copies, waits for them, and re-layouts: 61.3 us -> none  [the longest x1 30.8 us: route_local(): dest_slot = jnp.zeros((tok_dev,), jnp.int32).at[order_row].set(ranked_slot)]
    ppermute x0 -> x12, waiting for transfers between devices: none -> 43.4 us  [share(): out.append(lax.ppermute(w, EXPERT_AXES, pairs))]
    all_to_all x2 -> x0, starting transfers between devices: 22.5 us -> none  [the longest x1 13.3 us: device_step(): lax.all_to_all(expert_rows.reshape(num_experts, capacity, model_width), E...]
    ppermute x0 -> x12, starting transfers between devices: none -> 17.3 us  [share(): out.append(lax.ppermute(w, EXPERT_AXES, pairs))]
  transfers between devices with their start and end apart: 2 -> 12, of which waited for: 2 -> 5; matrix products, arithmetic and copies ran while one was open for 8% -> 5% of each run, Pallas kernels for 0% -> 18%
where the time goes in v1:
time: 246 us; the launch traced here: 241 us
  Pallas kernels  159 us (65%)
  waiting for transfers between devices  43.4 us (18%)
  starting transfers between devices  17.3 us (7%)
  matrix products  10.1 us (4%)
  local copies, waits for them, and re-layouts  8.89 us (4%)
    pallas_call x1, Pallas kernels, exchange(): pl.pallas_call(functools.partial(exchange_kernel, dims), name='exchange',...  97.5 us
    pallas_call x1, Pallas kernels, dispatch(): pl.pallas_call(functools.partial(dispatch_kernel, dims), name='dispatch',...  44.2 us
    ppermute x12, waiting for transfers between devices, share(): out.append(lax.ppermute(w, EXPERT_AXES, pairs))  43.4 us
    ppermute x12, starting transfers between devices, share(): out.append(lax.ppermute(w, EXPERT_AXES, pairs))  17.3 us
    pallas_call x1, Pallas kernels, combine(): pl.pallas_call(combine_kernel, name='combine', grid=(tok_dev // block,),...  17.2 us
    unnamed x34, local copies, waits for them, and re-layouts  8.87 us
    dot_general x1, matrix products, gates(): projected = jnp.dot(tok_rows, w_route, preferred_element_type=F32)  5.71 us
  transfers between devices with their start and end apart: 12, of which 5 were waited for; matrix products, arithmetic and copies ran while one was open for 5% of the time, Pallas kernels for 18%

profile of v1, /device:TPU:97, one launch (start us, length us, event | category | flops | bytes accessed | tf_op | source)
XLA Modules:
  0.0 241.3 jit_solution(4356207632889946724)
XLA Ops:
  0.0 0.0 copy-start
  0.0 3.7 %collective-permute-start.6 = (bf16[1,1,1536]{2,1,0:T(2,128)(2,1)}, bf16[1,1,1536]{2,1,0:T(2,128)(2,1)S(1)}, u32[]{:S(2)}, u32[]{:S(2)}) collective-permute-start(bf16[1,1,1536]{2,1,0:T(2,128)(2,1)} %bitcast.18), channel_id=1, source_target_pairs={{0,24},{1,7},{2,26},{3,1},{4,28},{5,3},{6,30},{7,5},{8,0},{9,15},{... | collective-permute-start | bytes 9224 | tf_op jit(solution)/shard_map/ppermute | solution.py:443
  3.7 0.2 collective-permute-start.7
  4.0 2.7 %collective-permute-start.10 = (bf16[1,1,384]{2,1,0:T(2,128)(2,1)}, bf16[1,1,384]{2,1,0:T(2,128)(2,1)S(1)}, u32[]{:S(2)}, u32[]{:S(2)}) collective-permute-start(bf16[1,1,384]{2,1,0:T(2,128)(2,1)} %bitcast.22), channel_id=1, source_target_pairs={{0,16},{1,5},{2,18},{3,7},{4,20},{5,1},{6,22},{7,3},{8,24},{9,13},... | collective-permute-start | bytes 2312 | tf_op jit(solution)/shard_map/ppermute | solution.py:443
  6.7 0.0 collective-permute-start.11
  6.7 2.7 %collective-permute-start = (bf16[1,384,1536]{2,1,0:T(8,128)(2,1)}, bf16[1,384,1536]{2,1,0:T(8,128)(2,1)}, u32[]{:S(2)}, u32[]{:S(2)}) collective-permute-start(bf16[1,384,1536]{2,1,0:T(8,128)(2,1)} %refs_0_.1), channel_id=1, source_target_pairs={{0,24},{1,7},{2,26},{3,1},{4,28},{5,3},{6,30},{7,5},{8,0},{9,15},{... | collective-permute-start | bytes 3538952 | tf_op jit(solution)/shard_map/ppermute | solution.py:443
  9.4 2.8 %copy-done.1 = bf16[1,8192,384]{2,1,0:T(8,128)(2,1)S(1)} copy-done((bf16[1,8192,384]{2,1,0:T(8,128)(2,1)S(1)}, bf16[1,8192,384]{2,1,0:T(8,128)(2,1)}, u32[]{:S(2)}) %copy-start.1) | copy-done | bytes 6291480
  12.2 0.8 copy-done.2
  12.9 0.8 copy-done.4
  13.7 44.2 %dispatch.1 = (bf16[10240,384]{1,0:T(8,128)(2,1)S(1)}, s32[64,128]{1,0:T(8,128)S(1)}) custom-call(s32[64,128]{1,0:T(8,128)S(1)} %bitcast.14, s32[64,128]{1,0:T(8,128)S(1)} %bitcast.17, bf16[8192,384]{1,0:T(8,128)(2,1)S(1)} %bitcast.13), custom_call_target="tpu_custom_call" | custom-call | flops 20000000000 | bytes 15000000 | tf_op jit(solution)/shard_map/dispatch/pallas_call | solution.py:132
  57.9 0.0 copy-start.8
  57.9 0.0 copy-start.9
  57.9 0.0 copy-start.7
  57.9 0.0 copy-start.10
  57.9 0.0 copy-start.11
  57.9 5.7 %multiply_reduce_fusion = (f32[8192]{0:T(1024)S(1)}, f32[8192,256]{0,1:T(8,128)}) fusion(bf16[384,256]{1,0:T(8,128)(2,1)S(1)} %copy-done, bf16[1,8192,384]{2,1,0:T(8,128)(2,1)S(1)} %copy-done.1), kind=kOutput, calls=%fused_computation.1 | convolution fusion | flops 1614798848 | bytes 14909440 | tf_op jit(solution)/shard_map/dot_general | solution.py:422
  63.7 0.3 copy-done.6
  63.9 0.0 collective-permute-done.10
  63.9 0.0 collective-permute-start.8
  63.9 0.0 collective-permute-done.11
  63.9 0.0 copy-done.9
  64.0 2.7 %collective-permute-start.9 = (bf16[1,1,384]{2,1,0:T(2,128)(2,1)S(1)}, bf16[1,1,384]{2,1,0:T(2,128)(2,1)S(1)}, u32[]{:S(2)}, u32[]{:S(2)}) collective-permute-start(bf16[1,1,384]{2,1,0:T(2,128)(2,1)S(1)} %bitcast.24), channel_id=1, source_target_pairs={{0,24},{1,7},{2,26},{3,1},{4,28},{5,3},{6,30},{7,5},{8,0},{9,15},{... | collective-permute-start | bytes 2312 | tf_op jit(solution)/shard_map/ppermute | solution.py:443
  66.6 0.1 fusion.3
  67.4 0.0 collective-permute-done.9
  67.4 1.3 collective-permute-start.1
  68.8 0.0 collective-permute-done.6
  68.8 2.1 collective-permute-start.2
  70.8 0.0 collective-permute-done.7
  70.8 0.6 collective-permute-start.3
  71.5 0.0 collective-permute-done.8
  71.5 1.3 collective-permute-start.4
  72.7 0.0 collective-permute-done.refs_1_
  72.7 0.0 collective-permute-start.5
  72.8 4.4 %fusion.7 = (f32[8192]{0:T(1024)S(1)}, f32[8192,32]{0,1:T(8,128)S(1)}) fusion(f32[]{:T(128)S(6)} %copy.11, bf16[32,256]{1,0:T(8,128)(2,1)S(1)} %copy-done.7, f32[32]{0:T(128)S(1)} %sqrt.17, f32[8192,256]{0,1:T(8,128)} %get-tuple-element.10, f32[8192]{0:T(1024)S(1)} %sqrt.16), kind=kOutput, calls=%fused_computation.16 | convolution fusion | flops 136847360 | bytes 9519236 | tf_op jit(solution)/shard_map/dot_general | solution.py:424
  77.2 0.2 fusion.2
  77.4 0.3 select_reduce_fusion
  77.7 0.6 pad_maximum_fusion.1.refs_9_
  78.3 0.6 pad_maximum_fusion.refs_8_
  79.0 5.5 %collective-permute-done.1.refs_2_ = bf16[1,384,1536]{2,1,0:T(8,128)(2,1)S(1)} collective-permute-done((bf16[1,384,1536]{2,1,0:T(8,128)(2,1)S(1)}, bf16[1,384,1536]{2,1,0:T(8,128)(2,1)S(1)}, u32[]{:S(2)}, u32[]{:S(2)}) %collective-permute-start.1) | collective-permute-done | bytes 1179680 | tf_op jit(solution)/shard_map/ppermute | solution.py:443
  84.4 12.6 %collective-permute-done.2.refs_3_ = bf16[1,384,1536]{2,1,0:T(8,128)(2,1)S(1)} collective-permute-done((bf16[1,384,1536]{2,1,0:T(8,128)(2,1)S(1)}, bf16[1,384,1536]{2,1,0:T(8,128)(2,1)S(1)}, u32[]{:S(2)}, u32[]{:S(2)}) %collective-permute-start.2) | collective-permute-done | bytes 1179680 | tf_op jit(solution)/shard_map/ppermute | solution.py:443
  97.0 0.4 collective-permute-done.3.refs_5_
  97.4 12.4 %collective-permute-done.4.refs_6_ = bf16[1,1536,384]{2,1,0:T(8,128)(2,1)S(1)} collective-permute-done((bf16[1,1536,384]{2,1,0:T(8,128)(2,1)S(1)}, bf16[1,1536,384]{2,1,0:T(8,128)(2,1)S(1)}, u32[]{:S(2)}, u32[]{:S(2)}) %collective-permute-start.4) | collective-permute-done | bytes 1179680 | tf_op jit(solution)/shard_map/ppermute | solution.py:443
  109.8 12.5 %collective-permute-done.5.refs_7_ = bf16[1,1536,384]{2,1,0:T(8,128)(2,1)S(1)} collective-permute-done((bf16[1,1536,384]{2,1,0:T(8,128)(2,1)S(1)}, bf16[1,1536,384]{2,1,0:T(8,128)(2,1)S(1)}, u32[]{:S(2)}, u32[]{:S(2)}) %collective-permute-start.5) | collective-permute-done | bytes 1179680 | tf_op jit(solution)/shard_map/ppermute | solution.py:443
  122.3 0.0 copy-done.14
  122.3 1.0 copy-done.16
  123.3 97.5 %exchange.1.back_hbm = bf16[10240,384]{1,0:T(8,128)(2,1)} custom-call(bf16[10240,384]{1,0:T(8,128)(2,1)} %copy-done.6, bf16[1,384,1536]{2,1,0:T(8,128)(2,1)} %refs_0_.1, bf16[1,384,1536]{2,1,0:T(8,128)(2,1)} %collective-permute-done.refs_1_, bf16[1,384,1536]{2,1,0:T(8,128)(2,1)} %copy-done.12, bf16[1,384,1536]{2,1,0:T(8,128)(2,1)} %copy-done.13, ...), custom_call_target="tpu_custom_call" | custom-call | flops 24159191040 | bytes 30000000 | tf_op jit(solution)/shard_map/exchange/pallas_call | solution.py:327
  220.8 3.2 %copy-done.5 = bf16[10240,384]{1,0:T(8,128)(2,1)S(1)} copy-done((bf16[10240,384]{1,0:T(8,128)(2,1)S(1)}, bf16[10240,384]{1,0:T(8,128)(2,1)}, u32[]{:S(2)}) %copy-start.5) | copy-done | bytes 7864344
  224.1 17.2 %combine.1 = bf16[8192,384]{1,0:T(8,128)(2,1)} custom-call(bf16[10240,384]{1,0:T(8,128)(2,1)S(1)} %copy-done.5, s32[64,128]{1,0:T(8,128)S(1)} %get-tuple-element.8.dest_sm, f32[64,128]{1,0:T(8,128)S(1)} %bitcast.16), custom_call_target="tpu_custom_call" | custom-call | flops 20000000000 | bytes 15000000 | tf_op jit(solution)/shard_map/combine/pallas_call | solution.py:400
  (22 shorter events, 0.1 us)
Async XLA Ops:
  0.0 57.9 %copy-start = (bf16[384,256]{1,0:T(8,128)(2,1)S(1)}, bf16[384,256]{1,0:T(8,128)(2,1)}, u32[]{:S(2)}) copy-start(bf16[384,256]{1,0:T(8,128)(2,1)} %param.13) | copy-start | bytes 589828
  0.0 68.8 %collective-permute-start.6 = (bf16[1,1,1536]{2,1,0:T(2,128)(2,1)}, bf16[1,1,1536]{2,1,0:T(2,128)(2,1)S(1)}, u32[]{:S(2)}, u32[]{:S(2)}) collective-permute-start(bf16[1,1,1536]{2,1,0:T(2,128)(2,1)} %bitcast.18), channel_id=1, source_target_pairs={{0,24},{1,7},{2,26},{3,1},{4,28},{5,3},{6,30},{7,5},{8,0},{9,15},{... | collective-permute-start | bytes 9224 | tf_op jit(solution)/shard_map/ppermute | solution.py:443
  3.7 67.1 %collective-permute-start.7 = (bf16[1,1,1536]{2,1,0:T(2,128)(2,1)}, bf16[1,1,1536]{2,1,0:T(2,128)(2,1)S(1)}, u32[]{:S(2)}, u32[]{:S(2)}) collective-permute-start(bf16[1,1,1536]{2,1,0:T(2,128)(2,1)} %bitcast.19), channel_id=1, source_target_pairs={{0,16},{1,5},{2,18},{3,7},{4,20},{5,1},{6,22},{7,3},{8,24},{9,13},... | collective-permute-start | bytes 9224 | tf_op jit(solution)/shard_map/ppermute | solution.py:443
  4.0 60.0 %collective-permute-start.10 = (bf16[1,1,384]{2,1,0:T(2,128)(2,1)}, bf16[1,1,384]{2,1,0:T(2,128)(2,1)S(1)}, u32[]{:S(2)}, u32[]{:S(2)}) collective-permute-start(bf16[1,1,384]{2,1,0:T(2,128)(2,1)} %bitcast.22), channel_id=1, source_target_pairs={{0,16},{1,5},{2,18},{3,7},{4,20},{5,1},{6,22},{7,3},{8,24},{9,13},... | collective-permute-start | bytes 2312 | tf_op jit(solution)/shard_map/ppermute | solution.py:443
  6.7 57.3 %collective-permute-start.11 = (bf16[1,1,384]{2,1,0:T(2,128)(2,1)}, bf16[1,1,384]{2,1,0:T(2,128)(2,1)S(1)}, u32[]{:S(2)}, u32[]{:S(2)}) collective-permute-start(bf16[1,1,384]{2,1,0:T(2,128)(2,1)} %bitcast.23), channel_id=1, source_target_pairs={{0,8},{1,3},{2,10},{3,5},{4,12},{5,7},{6,14},{7,1},{8,16},{9,11},{... | collective-permute-start | bytes 2312 | tf_op jit(solution)/shard_map/ppermute | solution.py:443
  6.7 66.1 %collective-permute-start = (bf16[1,384,1536]{2,1,0:T(8,128)(2,1)}, bf16[1,384,1536]{2,1,0:T(8,128)(2,1)}, u32[]{:S(2)}, u32[]{:S(2)}) collective-permute-start(bf16[1,384,1536]{2,1,0:T(8,128)(2,1)} %refs_0_.1), channel_id=1, source_target_pairs={{0,24},{1,7},{2,26},{3,1},{4,28},{5,3},{6,30},{7,5},{8,0},{9,15},{... | collective-permute-start | bytes 3538952 | tf_op jit(solution)/shard_map/ppermute | solution.py:443
  9.4 2.8 %copy-start.1 = (bf16[1,8192,384]{2,1,0:T(8,128)(2,1)S(1)}, bf16[1,8192,384]{2,1,0:T(8,128)(2,1)}, u32[]{:S(2)}) copy-start(bf16[1,8192,384]{2,1,0:T(8,128)(2,1)} %param.10) | copy-start | bytes 18874372
  12.1 0.8 copy-start.2
  12.9 0.8 copy-start.4
  57.9 6.0 %copy-start.6 = (bf16[10240,384]{1,0:T(8,128)(2,1)}, bf16[10240,384]{1,0:T(8,128)(2,1)S(1)}, u32[]{:S(2)}) copy-start(bf16[10240,384]{1,0:T(8,128)(2,1)S(1)} %get-tuple-element.7.send_hbm) | copy-start | bytes 23592964
  57.9 6.0 %copy-start.8 = (bf16[1,1536]{1,0:T(2,128)(2,1)S(1)}, bf16[1,1536]{1,0:T(2,128)(2,1)}, u32[]{:S(2)}) copy-start(bf16[1,1536]{1,0:T(2,128)(2,1)} %param.17) | copy-start | bytes 9220
  57.9 6.1 %copy-start.9 = (bf16[1,384]{1,0:T(2,128)(2,1)S(1)}, bf16[1,384]{1,0:T(2,128)(2,1)}, u32[]{:S(2)}) copy-start(bf16[1,384]{1,0:T(2,128)(2,1)} %param.19) | copy-start | bytes 2308
  57.9 8.7 %copy-start.7 = (bf16[32,256]{1,0:T(8,128)(2,1)S(1)}, bf16[32,256]{1,0:T(8,128)(2,1)}, u32[]{:S(2)}) copy-start(bf16[32,256]{1,0:T(8,128)(2,1)} %param.14) | copy-start | bytes 49156
  57.9 9.5 %copy-start.10 = (bf16[1,384,1536]{2,1,0:T(8,128)(2,1)S(1)}, bf16[1,384,1536]{2,1,0:T(8,128)(2,1)}, u32[]{:S(2)}) copy-start(bf16[1,384,1536]{2,1,0:T(8,128)(2,1)} %refs_0_.1) | copy-start | bytes 3538948
  57.9 12.9 %copy-start.11 = (bf16[1,1536,384]{2,1,0:T(8,128)(2,1)S(1)}, bf16[1,1536,384]{2,1,0:T(8,128)(2,1)}, u32[]{:S(2)}) copy-start(bf16[1,1536,384]{2,1,0:T(8,128)(2,1)} %refs_4_.1) | copy-start | bytes 3538948
  63.9 7.5 %collective-permute-start.8 = (bf16[1,1,1536]{2,1,0:T(2,128)(2,1)S(1)}, bf16[1,1,1536]{2,1,0:T(2,128)(2,1)S(1)}, u32[]{:S(2)}, u32[]{:S(2)}) collective-permute-start(bf16[1,1,1536]{2,1,0:T(2,128)(2,1)S(1)} %bitcast.20), channel_id=1, source_target_pairs={{0,8},{1,3},{2,10},{3,5},{4,12},{5,7},{6,14},{7,1},{8,16},{9,11},{... | collective-permute-start | bytes 9224 | tf_op jit(solution)/shard_map/ppermute | solution.py:443
  64.0 3.5 %collective-permute-start.9 = (bf16[1,1,384]{2,1,0:T(2,128)(2,1)S(1)}, bf16[1,1,384]{2,1,0:T(2,128)(2,1)S(1)}, u32[]{:S(2)}, u32[]{:S(2)}) collective-permute-start(bf16[1,1,384]{2,1,0:T(2,128)(2,1)S(1)} %bitcast.24), channel_id=1, source_target_pairs={{0,24},{1,7},{2,26},{3,1},{4,28},{5,3},{6,30},{7,5},{8,0},{9,15},{... | collective-permute-start | bytes 2312 | tf_op jit(solution)/shard_map/ppermute | solution.py:443
  67.4 17.0 %collective-permute-start.1 = (bf16[1,384,1536]{2,1,0:T(8,128)(2,1)S(1)}, bf16[1,384,1536]{2,1,0:T(8,128)(2,1)S(1)}, u32[]{:S(2)}, u32[]{:S(2)}) collective-permute-start(bf16[1,384,1536]{2,1,0:T(8,128)(2,1)S(1)} %copy-done.10), channel_id=1, source_target_pairs={{0,16},{1,5},{2,18},{3,7},{4,20},{5,1},{6,22},{7,3},{8,24},{9,13},... | collective-permute-start | bytes 3538952 | tf_op jit(solution)/shard_map/ppermute | solution.py:443
  68.8 28.3 %collective-permute-start.2 = (bf16[1,384,1536]{2,1,0:T(8,128)(2,1)S(1)}, bf16[1,384,1536]{2,1,0:T(8,128)(2,1)S(1)}, u32[]{:S(2)}, u32[]{:S(2)}) collective-permute-start(bf16[1,384,1536]{2,1,0:T(8,128)(2,1)S(1)} %copy-done.10), channel_id=1, source_target_pairs={{0,8},{1,3},{2,10},{3,5},{4,12},{5,7},{6,14},{7,1},{8,16},{9,11},{... | collective-permute-start | bytes 3538952 | tf_op jit(solution)/shard_map/ppermute | solution.py:443
  70.8 26.6 %collective-permute-start.3 = (bf16[1,1536,384]{2,1,0:T(8,128)(2,1)S(1)}, bf16[1,1536,384]{2,1,0:T(8,128)(2,1)S(1)}, u32[]{:S(2)}, u32[]{:S(2)}) collective-permute-start(bf16[1,1536,384]{2,1,0:T(8,128)(2,1)S(1)} %copy-done.11), channel_id=1, source_target_pairs={{0,24},{1,7},{2,26},{3,1},{4,28},{5,3},{6,30},{7,5},{8,0},{9,15},{... | collective-permute-start | bytes 3538952 | tf_op jit(solution)/shard_map/ppermute | solution.py:443
  71.5 38.3 %collective-permute-start.4 = (bf16[1,1536,384]{2,1,0:T(8,128)(2,1)S(1)}, bf16[1,1536,384]{2,1,0:T(8,128)(2,1)S(1)}, u32[]{:S(2)}, u32[]{:S(2)}) collective-permute-start(bf16[1,1536,384]{2,1,0:T(8,128)(2,1)S(1)} %copy-done.11), channel_id=1, source_target_pairs={{0,16},{1,5},{2,18},{3,7},{4,20},{5,1},{6,22},{7,3},{8,24},{9,13},... | collective-permute-start | bytes 3538952 | tf_op jit(solution)/shard_map/ppermute | solution.py:443
  72.7 49.6 %collective-permute-start.5 = (bf16[1,1536,384]{2,1,0:T(8,128)(2,1)S(1)}, bf16[1,1536,384]{2,1,0:T(8,128)(2,1)S(1)}, u32[]{:S(2)}, u32[]{:S(2)}) collective-permute-start(bf16[1,1536,384]{2,1,0:T(8,128)(2,1)S(1)} %copy-done.11), channel_id=1, source_target_pairs={{0,8},{1,3},{2,10},{3,5},{4,12},{5,7},{6,14},{7,1},{8,16},{9,11},{... | collective-permute-start | bytes 3538952 | tf_op jit(solution)/shard_map/ppermute | solution.py:443
  72.7 4.6 %copy-start.3 = (s32[1,8192]{1,0:T(1,128)S(1)}, s32[1,8192]{1,0:T(1,128)}, u32[]{:S(2)}) copy-start(s32[1,8192]{1,0:T(1,128)} %param.11) | copy-start | bytes 98308
  84.4 37.9 %copy-start.12 = (bf16[1,384,1536]{2,1,0:T(8,128)(2,1)}, bf16[1,384,1536]{2,1,0:T(8,128)(2,1)S(1)}, u32[]{:S(2)}) copy-start(bf16[1,384,1536]{2,1,0:T(8,128)(2,1)S(1)} %collective-permute-done.1.refs_2_) | copy-start | bytes 3538948
  97.0 25.3 %copy-start.13 = (bf16[1,384,1536]{2,1,0:T(8,128)(2,1)}, bf16[1,384,1536]{2,1,0:T(8,128)(2,1)S(1)}, u32[]{:S(2)}) copy-start(bf16[1,384,1536]{2,1,0:T(8,128)(2,1)S(1)} %collective-permute-done.2.refs_3_) | copy-start | bytes 3538948
  97.4 24.9 %copy-start.14 = (bf16[1,1536,384]{2,1,0:T(8,128)(2,1)}, bf16[1,1536,384]{2,1,0:T(8,128)(2,1)S(1)}, u32[]{:S(2)}) copy-start(bf16[1,1536,384]{2,1,0:T(8,128)(2,1)S(1)} %collective-permute-done.3.refs_5_) | copy-start | bytes 3538948
  109.8 12.6 %copy-start.15 = (bf16[1,1536,384]{2,1,0:T(8,128)(2,1)}, bf16[1,1536,384]{2,1,0:T(8,128)(2,1)S(1)}, u32[]{:S(2)}) copy-start(bf16[1,1536,384]{2,1,0:T(8,128)(2,1)S(1)} %collective-permute-done.4.refs_6_) | copy-start | bytes 3538948
  122.3 1.0 copy-start.16
  220.8 3.2 %copy-start.5 = (bf16[10240,384]{1,0:T(8,128)(2,1)S(1)}, bf16[10240,384]{1,0:T(8,128)(2,1)}, u32[]{:S(2)}) copy-start(bf16[10240,384]{1,0:T(8,128)(2,1)} %exchange.1.back_hbm) | copy-start | bytes 23592964

commit v2 on v0

v2 whole, which is shorter than its diff:
```python
import functools

import jax
import jax.numpy as jnp
from jax import lax
from jax.experimental import pallas as pl
from jax.experimental.pallas import tpu as pltpu
from jax.sharding import PartitionSpec as P

EXPERT_AXES = ("ep_b", "ep_a")
LANES = 128
MESH_ID = pl.DeviceIdType.MESH
F32 = jnp.float32
BF16 = jnp.bfloat16


def iota(shape, dim):
    return lax.broadcasted_iota(jnp.int32, shape, dim)


def dot_nt(a, b):
    return lax.dot_general(a, b, (((1,), (1,)), ((), ())), preferred_element_type=F32)


def as_bf16(mask):
    return jnp.where(mask, 1.0, 0.0).astype(BF16)


def virtual_expert(ids, size_b, size_x):
    i_b, i_a = ids // (2 * size_x), ids % (2 * size_x)
    x, core = i_a // 2, i_a % 2
    return jnp.where(core == 0, x * size_b + i_b, size_b * size_x + i_b * size_x + x)


def route_kernel(dims, parts, ids_ref, order_ref, src_ref, dest_ref):
    size_b, size_x, cap = dims
    rows, slot_rows = ids_ref.shape[0], src_ref.shape[0]
    num_experts = 2 * size_b * size_x
    upper = as_bf16((iota((LANES, 2 * LANES), 0) <= iota((LANES, 2 * LANES), 1)) | (iota((LANES, 2 * LANES), 1) >= LANES))
    ids_t = ids_ref[...].astype(F32).T.astype(BF16)
    iota_rows = iota((rows, LANES), 0)
    iota_lane = iota((LANES, LANES), 0)
    iota_exp = iota((num_experts, LANES), 0)

    def ranked(r, carry):
        count, keep = carry
        o = order_ref[pl.ds(r, 1), :]
        pick_hi = iota_rows == o // LANES
        pick_lo = iota_lane == o % LANES
        table = jnp.dot(ids_t, as_bf16(pick_hi), preferred_element_type=F32)
        rid = jnp.sum(jnp.where(pick_lo, table, 0.0), axis=0, keepdims=True)
        mine = iota_exp.astype(F32) == rid
        both = jnp.dot(as_bf16(mine), upper, preferred_element_type=F32)
        rank = jnp.sum(jnp.where(mine, both[:, :LANES] + count, 0.0), axis=0, keepdims=True)
        keep = keep + dot_nt(as_bf16(pick_hi & (rank <= float(cap))), as_bf16(pick_lo))
        return count + both[:, LANES:], keep

    zero_count = jnp.zeros((num_experts, LANES), F32)
    _, keep = lax.fori_loop(0, rows, ranked, (zero_count, jnp.zeros((rows, LANES), F32)), unroll=8)
    dest_ref[...] = keep.astype(jnp.int32)

    iota_slot = iota((slot_rows, LANES), 0)
    lane = iota((1, LANES), 1).astype(F32)

    def placed(r, carry):
        count, source = carry
        expert = virtual_expert(ids_ref[pl.ds(r, 1), :], size_b, size_x)
        kept = dest_ref[pl.ds(r, 1), :] > 0
        mine = (iota_exp == expert) & kept
        both = jnp.dot(as_bf16(mine), upper, preferred_element_type=F32)
        place = jnp.sum(jnp.where(mine, both[:, :LANES] + count, 0.0), axis=0, keepdims=True) - 1.0
        slot = jnp.where(kept, expert * cap + place.astype(jnp.int32), num_experts * cap)
        dest_ref[pl.ds(r, 1), :] = slot * parts
        hit = jnp.where(iota_slot == slot // LANES, 1.0, 0.0)
        stacked = jnp.concatenate([hit * lax.convert_element_type(r, F32), hit * lane], axis=0).astype(BF16)
        source = source + dot_nt(stacked, as_bf16(iota_lane == slot % LANES))
        return count + both[:, LANES:], source

    _, source = lax.fori_loop(0, rows, placed, (zero_count, jnp.zeros((2 * slot_rows, LANES), F32)), unroll=4)
    src_ref[...] = ((source[:slot_rows] * float(LANES) + source[slot_rows:]) * float(parts)).astype(jnp.int32)


def route(ids, order, dims, parts):
    size_b, size_x, cap = dims
    slot_rows = 2 * size_b * size_x * cap // LANES
    return pl.pallas_call(
        functools.partial(route_kernel, dims, parts),
        name="route",
        out_shape=(jax.ShapeDtypeStruct((slot_rows, LANES), jnp.int32), jax.ShapeDtypeStruct(ids.shape, jnp.int32)),
        cost_estimate=pl.CostEstimate(flops=5_000_000_000, bytes_accessed=200_000, transcendentals=0),
    )(ids, order)


def pick(table, t):
    value = jnp.int32(0)
    for i, entry in enumerate(table):
        if entry:
            value = value + jnp.where(t == i, entry, 0)
    return value


def experts_kernel(dims, ids_ref, src_sm, wr_ref, keys_ref, tau_ref, bias_hbm, tok_hbm, w1_hbm, w2_hbm,
                   back_hbm, gate_ref,
                   tok_vm, big, tmp, send, recv, w1, w2, bias,
                   tok_sem, wout_sem, win_sem, out_sem, in_sem, ret_sem, back_sem):
    size_b, size_x, cap = dims
    n = size_x
    rows = ids_ref.shape[0]
    num_experts = 2 * size_b * size_x
    parts = tok_vm.shape[1] // LANES
    i_dp, i_b, i_a = lax.axis_index("dp"), lax.axis_index("ep_b"), lax.axis_index("ep_a")
    pos_x, core, pos_y = i_a // 2, lax.rem(i_a, 2), i_b
    pos = (1 - core) * pos_x + core * pos_y
    wpos = (1 - core) * pos_y + core * pos_x

    def sends_to(kind, k):
        return i_dp, (1 - kind) * pos_y + kind * k, 2 * ((1 - kind) * k + kind * pos_x) + kind

    def serves(k, c):
        return i_dp, core * k + (1 - core) * pos_y, 2 * (core * pos_x + (1 - core) * k) + c

    def shares(k):
        return i_dp, (1 - core) * k + core * pos_y, 2 * ((1 - core) * pos_x + core * k) + core

    def block(i):
        return pl.ds(pl.multiple_of(i * cap, cap), cap)

    tok_copy = pltpu.make_async_copy(tok_hbm, tok_vm, tok_sem)
    tok_copy.start()
    held = ((w1_hbm, w1), (w2_hbm, w2), (bias_hbm, bias))
    for i, (own, every) in enumerate(held):
        pltpu.make_async_copy(own, every.at[pl.ds(0, 1)], win_sem.at[i, 0]).start()

    barrier = pltpu.get_barrier_semaphore()
    for k in range(n):
        for c in range(2):
            for device in (sends_to(c, k), serves(k, c)):
                pl.semaphore_signal(barrier, inc=1, device_id=device, device_id_type=MESH_ID)
    for d in range(1, n):
        pl.semaphore_signal(barrier, inc=1, device_id=shares(lax.rem(wpos + d, n)), device_id_type=MESH_ID)
    pl.semaphore_wait(barrier, 5 * n - 1)

    def weight_copy(i, d):
        own, every = held[i]
        return pltpu.make_async_remote_copy(
            src_ref=own, dst_ref=every.at[pl.ds(d, 1)], send_sem=wout_sem.at[i, d], recv_sem=win_sem.at[i, d],
            device_id=shares(lax.rem(wpos - d + n, n)), device_id_type=MESH_ID)

    weight_order = [1, n - 1] + list(range(2, n - 1))
    for d in weight_order:
        for i in (2, 0, 1):
            weight_copy(i, d).start()

    iota_exp = iota((num_experts, LANES), 0)

    tok_copy.wait()

    def widen(i, _):
        base = pl.multiple_of(i * 16, 16)
        for c in range(parts):
            big[pl.ds(base * parts + c, 16, stride=parts), :] = tok_vm[pl.ds(base, 16), c * LANES:(c + 1) * LANES].astype(F32)
        return 0

    lax.fori_loop(0, tok_vm.shape[0] // 16, widen, 0, unroll=8)

    near, far = [1, n - 1], list(range(2, n - 1))
    send_order = [(step, off, kind) for group in (near, far, [0]) for off in range(n) for step in group for kind in range(2)]

    def outgoing(t):
        step, off, kind = (pick([e[i] for e in send_order], t) for i in range(3))
        k = lax.rem((1 - kind) * pos_x + kind * pos_y + step, n)
        j = lax.rem((1 - kind) * pos_y + kind * pos_x + off, n)
        return step, kind, k, j

    def send_block(t):
        step, kind, k, j = outgoing(t)
        src = (kind * n + k) * n + j
        dst = (((1 - kind) * pos_x + kind * pos_y) * n + j) * 2 + core
        own = (step == 0) & (kind == core)

        @pl.when(own)
        def _():
            pltpu.make_async_copy(send.at[block(src)], recv.at[block(dst)], in_sem.at[dst]).start()

        @pl.when(jnp.logical_not(own))
        def _():
            pltpu.make_async_remote_copy(
                src_ref=send.at[block(src)], dst_ref=recv.at[block(dst)], send_sem=out_sem.at[src], recv_sem=in_sem.at[dst],
                device_id=sends_to(kind, k), device_id_type=MESH_ID).start()

    group_rows = 64 if cap % 64 == 0 else 16

    def gather_block(t, _):
        _, kind, k, j = outgoing(t)
        base = ((kind * n + k) * n + j) * cap

        def gather(g, _):
            first = pl.multiple_of(base + g * group_rows, group_rows)
            row, col = first // LANES, lax.rem(first, LANES)
            for u in range(group_rows):
                tmp[pl.ds(u * parts, parts), :] = big[pl.ds(src_sm[row, col + u], parts), :]
            for u in range(0, group_rows, 16):
                for c in range(parts):
                    send[pl.ds(pl.multiple_of(first + u, 16), 16), c * LANES:(c + 1) * LANES] = (
                        tmp[pl.ds(u * parts + c, 16, stride=parts), :].astype(BF16))
            return 0

        lax.fori_loop(0, cap // group_rows, gather, 0)

        @pl.when(t > 0)
        def _():
            send_block(t - 1)
        return 0

    blocks = 2 * n * n
    lax.fori_loop(0, blocks, gather_block, 0)

    keys = keys_ref[...].astype(F32)
    key_unit = keys / jnp.sqrt(jnp.sum(keys * keys, axis=1, keepdims=True))
    tau = tau_ref[0, 0]
    ones = jnp.ones((8, wr_ref.shape[1]), F32)
    span = 4

    def gate_rows(i, _):
        x = tok_vm[pl.ds(pl.multiple_of(i * span * LANES, span * LANES), span * LANES), :]
        r = jnp.dot(x, wr_ref[...], preferred_element_type=F32)
        exact = dict(preferred_element_type=F32, precision=lax.Precision.HIGHEST)
        dots = lax.dot_general(key_unit, r, (((1,), (1,)), ((), ())), **exact)
        norm = jnp.sqrt(lax.dot_general(ones, r * r, (((1,), (1,)), ((), ())), **exact)[:1])
        logits = dots / norm / tau
        p = jnp.exp(logits - jnp.max(logits, axis=0, keepdims=True))
        total = jnp.sum(p, axis=0, keepdims=True)
        for q in range(span):
            mine = iota_exp == ids_ref[pl.ds(i * span + q, 1), :]
            cols = slice(q * LANES, (q + 1) * LANES)
            gate_ref[pl.ds(i * span + q, 1), :] = jnp.sum(jnp.where(mine, p[:, cols], 0.0), axis=0, keepdims=True) / total[:, cols]
        return 0

    send_block(jnp.int32(blocks - 1))
    lax.fori_loop(0, rows // span, gate_rows, 0)

    serve_order = ([(0, off) for off in range(n // 2)] + [(step, off) for off in range(n) for step in near]
                   + [(0, off) for off in range(n // 2, n - 1)] + [(step, off) for step in far for off in range(n)] + [(0, n - 1)])
    first_use = [int(off not in [o for _, o in serve_order[:i]]) for i, (_, off) in enumerate(serve_order)]

    def incoming(t):
        step, off = (pick([e[i] for e in serve_order], t) for i in range(2))
        return lax.rem(pos - step + n, n), off, lax.rem(wpos + off, n)

    def result_ends(t, c):
        k, _, j = incoming(t)
        src, dst = (k * n + j) * 2 + c, (core * n + pos) * n + j
        return k, src, dst, (k == pos) & (core == c)

    def send_results(t):
        for c in range(2):
            k, src, dst, own = result_ends(t, c)

            @pl.when(own)
            def _():
                pltpu.make_async_copy(recv.at[block(src)], back_hbm.at[block(dst)], back_sem.at[dst]).start()

            @pl.when(jnp.logical_not(own))
            def _():
                pltpu.make_async_remote_copy(
                    src_ref=recv.at[block(src)], dst_ref=back_hbm.at[block(dst)], send_sem=ret_sem.at[src],
                    recv_sem=back_sem.at[dst], device_id=serves(k, c), device_id_type=MESH_ID).start()

    def serve(t, _):
        k, off, j = incoming(t)
        first = (k * n + j) * 2

        @pl.when(pick(first_use, t) == 1)
        def _():
            for i, (own, every) in enumerate(held):
                pltpu.make_async_copy(own, every.at[pl.ds(off, 1)], win_sem.at[i, off]).wait()

        for c in range(2):
            pltpu.make_async_copy(send.at[block(0)], recv.at[block(first + c)], in_sem.at[first + c]).wait()
        here = pl.ds(pl.multiple_of(first * cap, 2 * cap), 2 * cap)
        hidden = jnp.dot(recv[here, :], w1[off], preferred_element_type=F32) + bias[off, 0:1, :].astype(F32)
        hidden = (0.5 * hidden * (1.0 + lax.erf(hidden * (0.5 ** 0.5)))).astype(BF16)
        y = jnp.dot(hidden, w2[off], preferred_element_type=F32) + bias[off, 1:2, :recv.shape[1]].astype(F32)
        recv[here, :] = y.astype(BF16)

        @pl.when(t > 0)
        def _():
            send_results(t - 1)
        return 0

    lax.fori_loop(0, n * n, serve, 0)
    send_results(jnp.int32(n * n - 1))

    for d in range(1, n):
        for i in range(3):
            weight_copy(i, d).wait_send()

    def drain(t, _):
        sent = pltpu.make_async_remote_copy(
            src_ref=send.at[block(t)], dst_ref=recv.at[block(t)], send_sem=out_sem.at[t], recv_sem=in_sem.at[t],
            device_id=(i_dp, i_b, i_a), device_id_type=MESH_ID)
        returned = pltpu.make_async_remote_copy(
            src_ref=recv.at[block(t)], dst_ref=back_hbm.at[block(t)], send_sem=ret_sem.at[t], recv_sem=back_sem.at[t],
            device_id=(i_dp, i_b, i_a), device_id_type=MESH_ID)
        kind, k = t // (n * n), lax.rem(t // n, n)

        @pl.when((kind != core) | (k != pos))
        def _():
            sent.wait_send()

        @pl.when((t // (2 * n) != pos) | (lax.rem(t, 2) != core))
        def _():
            returned.wait_send()

        returned.wait_recv()
        return 0

    lax.fori_loop(0, blocks, drain, 0)


def experts(tok_rows, ids, source, w_route, expert_keys, temperature, w1, w2, bias, dims):
    size_b, size_x, cap = dims
    n = size_x
    tok_dev, width = tok_rows.shape
    hidden = w1.shape[2]
    slots = 2 * size_b * size_x * cap
    rows, parts = tok_dev // LANES, width // LANES
    vmem, smem, hbm = (pl.BlockSpec(memory_space=m) for m in (pltpu.VMEM, pltpu.SMEM, pltpu.HBM))
    dma = pltpu.SemaphoreType.DMA
    return pl.pallas_call(
        functools.partial(experts_kernel, dims),
        name="experts",
        out_shape=(jax.ShapeDtypeStruct((slots, width), BF16), jax.ShapeDtypeStruct((rows, LANES), F32)),
        in_specs=[vmem, smem, vmem, vmem, smem] + [hbm] * 4,
        out_specs=(hbm, vmem),
        scratch_shapes=[
            pltpu.VMEM((tok_dev, width), BF16),
            pltpu.VMEM((tok_dev * parts + 8, LANES), F32),
            pltpu.VMEM((64 * parts + 8, LANES), F32),
            pltpu.VMEM((slots, width), BF16),
            pltpu.VMEM((slots, width), BF16),
            pltpu.VMEM((n, width, hidden), BF16),
            pltpu.VMEM((n, hidden, width), BF16),
            pltpu.VMEM((n,) + bias.shape[1:], BF16),
            dma, dma((3, n)), dma((3, n)),
            dma((2 * n * n,)), dma((2 * n * n,)), dma((2 * n * n,)), dma((2 * n * n,)),
        ],
        compiler_params=pltpu.CompilerParams(collective_id=1, has_side_effects=True, vmem_limit_bytes=60 << 20),
        cost_estimate=pl.CostEstimate(flops=4 * slots * width * hidden, bytes_accessed=30_000_000, transcendentals=0),
    )(ids, source, w_route, expert_keys, temperature.reshape(1, 1),
      bias, tok_rows, w1, w2)


def combine_kernel(back_hbm, dest_sm, gate_sm, out_ref, stage, big, tmp, sem):
    i = pl.program_id(0)
    slots, width = back_hbm.shape
    parts = width // LANES
    chunk = stage.shape[1]
    chunks = slots // chunk

    @pl.when(i == 0)
    def _():
        def fetch(q):
            return pltpu.make_async_copy(back_hbm.at[pl.ds(pl.multiple_of(q * chunk, chunk), chunk)], stage.at[lax.rem(q, 2)],
                                         sem.at[lax.rem(q, 2)])
        fetch(0).start()
        big[pl.ds(slots * parts, 8), :] = jnp.zeros((8, LANES), F32)

        def widen_chunk(q, _):
            @pl.when(q + 1 < chunks)
            def _():
                fetch(q + 1).start()
            fetch(q).wait()

            def widen(u, _):
                base = pl.multiple_of(u * 16, 16)
                for c in range(parts):
                    big[pl.ds((q * chunk + base) * parts + c, 16, stride=parts), :] = (
                        stage[lax.rem(q, 2), pl.ds(base, 16), c * LANES:(c + 1) * LANES].astype(F32))
                return 0

            lax.fori_loop(0, chunk // 16, widen, 0, unroll=8)
            return 0

        lax.fori_loop(0, chunks, widen_chunk, 0)

    def gather(g, _):
        row = i * (out_ref.shape[0] // LANES) + g
        for j in range(LANES):
            tmp[pl.ds(j * parts, parts), :] = big[pl.ds(dest_sm[row, j], parts), :] * gate_sm[row, j]
        for j in range(0, LANES, 16):
            for c in range(parts):
                out_ref[pl.ds(pl.multiple_of(g * LANES + j, 16), 16), c * LANES:(c + 1) * LANES] = (
                    tmp[pl.ds(j * parts + c, 16, stride=parts), :].astype(BF16))
        return 0

    lax.fori_loop(0, out_ref.shape[0] // LANES, gather, 0)


def combine(back_rows, dest, gate, tok_dev):
    slots, width = back_rows.shape
    parts = width // LANES
    block = 1024
    smem = pl.BlockSpec(memory_space=pltpu.SMEM)
    return pl.pallas_call(
        combine_kernel,
        name="combine",
        grid=(tok_dev // block,),
        out_shape=jax.ShapeDtypeStruct((tok_dev, width), BF16),
        in_specs=[pl.BlockSpec(memory_space=pltpu.HBM), smem, smem],
        out_specs=pl.BlockSpec((block, width), lambda i: (i, 0)),
        scratch_shapes=[
            pltpu.VMEM((2, 1280, width), BF16),
            pltpu.VMEM((slots * parts + 8, LANES), F32),
            pltpu.VMEM((LANES * parts, LANES), F32),
            pltpu.SemaphoreType.DMA((2,)),
        ],
        compiler_params=pltpu.CompilerParams(vmem_limit_bytes=40 << 20, dimension_semantics=("arbitrary",)),
        cost_estimate=pl.CostEstimate(flops=20_000_000_000, bytes_accessed=15_000_000, transcendentals=0),
    )(back_rows, dest, gate)


def solution(mesh):
    size_b, size_x = mesh.shape["ep_b"], mesh.shape["ep_a"] // 2
    num_experts = 2 * size_b * size_x
    tok_spec = P(("dp",) + EXPERT_AXES)
    expert_spec = P(EXPERT_AXES)

    def device_step(tokens, expert_ids, route_order, w_route, expert_keys, temperature, w_in, b_in, w_out, b_out):
        tok_dev = tokens.shape[1]
        cap = (5 * tok_dev + 4 * num_experts - 1) // (4 * num_experts)
        dims = (size_b, size_x, cap)
        widen = lambda b: jnp.pad(b, ((0, 0), (0, w_in.shape[2] - b.shape[1])))
        bias = jnp.pad(jnp.stack([b_in, widen(b_out)], axis=1), ((0, 0), (0, 14), (0, 0)))
        ids = expert_ids.reshape(tok_dev // LANES, LANES)
        source, dest = route(ids, route_order.reshape(ids.shape), dims, tokens.shape[2] // LANES)
        back_rows, gate = experts(tokens[0], ids, source, w_route, expert_keys, temperature, w_in, w_out, bias, dims)
        return combine(back_rows, dest, gate, tok_dev)[None]

    return jax.shard_map(
        device_step,
        mesh=mesh,
        in_specs=(tok_spec, tok_spec, tok_spec, P(), P(), P(), expert_spec, expert_spec, expert_spec, expert_spec),
        out_specs=tok_spec,
        check_vma=False,
    )
```

time: 575 us -> 198 us (0.34); the launches traced: 568 us -> 197 us
  Pallas kernels: 0 us -> 191 us
  matrix products: 184 us -> 0 us
  local copies, waits for them, and re-layouts: 181 us -> 4.68 us
  waiting for transfers between devices: 149 us -> 0 us
  other arithmetic: 30.3 us -> 1.33 us
  starting transfers between devices: 22.5 us -> 0 us
    pallas_call x0 -> x3, Pallas kernels: none -> 191 us  [the longest x1 150 us: experts(): pl.pallas_call(functools.partial(experts_kernel, dims), name='experts', o...]
    dot_general x4 -> x0, matrix products: 184 us -> none  [the longest x1 149 us: expert_local(): jnp.dot(slot_rows, w_first, preferred_element_type=jnp.float32)]
    all_to_all x2 -> x0, waiting for transfers between devices: 149 us -> none  [the longest x1 95.5 us: device_step(): lax.all_to_all(send_rows.reshape(num_experts, capacity, model_width), EXP...]
    gather x3 -> x0, local copies, waits for them, and re-layouts: 118 us -> none  [the longest x1 43.9 us: route_local(): jnp.take(tok_rows, slot_source, axis=0, mode='fill', fill_value=0)]
    scatter x2 -> x0, local copies, waits for them, and re-layouts: 61.3 us -> none  [the longest x1 30.8 us: route_local(): dest_slot = jnp.zeros((tok_dev,), jnp.int32).at[order_row].set(ranked_slot)]
    all_to_all x2 -> x0, starting transfers between devices: 22.5 us -> none  [the longest x1 13.3 us: device_step(): lax.all_to_all(expert_rows.reshape(num_experts, capacity, model_width), E...]
    convert_element_type x2 -> x0, other arithmetic: 9.19 us -> none  [the longest x1 9.08 us: combine_local(): (gate_prob[:, None] * picked.astype(jnp.float32)).astype(jnp.bfloat16)]
    select_n x6 -> x0, other arithmetic: 8.98 us -> none  [the longest x1 7.32 us: route_local(): jnp.take(tok_rows, slot_source, axis=0, mode='fill', fill_value=0)]
  transfers between devices with their start and end apart: 2 -> 0, of which waited for: 2 -> 0; matrix products, arithmetic and copies ran while one was open for 8% -> 0% of each run, Pallas kernels for 0% -> 0%
where the time goes in v2:
time: 198 us; the launch traced here: 197 us
  Pallas kernels  191 us (96%)
  local copies, waits for them, and re-layouts  4.68 us (2%)
    pallas_call x1, Pallas kernels, experts(): pl.pallas_call(functools.partial(experts_kernel, dims), name='experts', o...  150 us
    pallas_call x1, Pallas kernels, route(): pl.pallas_call(functools.partial(route_kernel, dims, parts), name='route'...  23.6 us
    pallas_call x1, Pallas kernels, combine(): pl.pallas_call(combine_kernel, name='combine', grid=(tok_dev // block,),...  17.2 us
    unnamed x6, local copies, waits for them, and re-layouts  3.99 us

profile of v2, /device:TPU:97, one launch (start us, length us, event | category | flops | bytes accessed | tf_op | source)
XLA Modules:
  0.0 197.2 jit_solution(14115273554713759966)
XLA Ops:
  0.7 0.7 pad_bitcast_fusion
  1.3 1.3 fusion.2.bias_hbm
  2.7 23.6 %route.1 = (s32[80,128]{1,0:T(8,128)}, s32[64,128]{1,0:T(8,128)}) custom-call(s32[64,128]{1,0:T(8,128)} %bitcast.12, s32[64,128]{1,0:T(8,128)} %bitcast.11), custom_call_target="tpu_custom_call" | custom-call | flops 5000000000 | bytes 200000 | tf_op jit(solution)/shard_map/route/pallas_call | solution.py:86
  26.3 0.0 copy-start.1
  26.3 149.7 %experts.1 = (bf16[10240,384]{1,0:T(8,128)(2,1)}, f32[64,128]{1,0:T(8,128)}) custom-call(s32[64,128]{1,0:T(8,128)} %bitcast.13, s32[80,128]{1,0:T(8,128)} %get-tuple-element.9.src_sm, bf16[384,256]{1,0:T(8,128)(2,1)} %wr_ref.1, bf16[32,256]{1,0:T(8,128)(2,1)} %keys_ref.1, f32[1,1]{1,0:T(1,128)} %bitcast.8.tau_ref, bf16[1,16,1536]{2,1,0:T(8,128)(2,1)} %fusion.2.bias_hbm, ...), custom_call_target="tpu_custom_call" | custom-call | flops 24159191040 | bytes 30000000 | tf_op jit(solution)/shard_map/experts/pallas_call | solution.py:330
  176.0 0.0 copy-done.1
  176.0 0.0 copy-start
  176.0 3.2 %copy-done = bf16[10240,384]{1,0:T(8,128)(2,1)S(1)} copy-done((bf16[10240,384]{1,0:T(8,128)(2,1)S(1)}, bf16[10240,384]{1,0:T(8,128)(2,1)}, u32[]{:S(2)}) %copy-start) | copy-done | bytes 7864344
  179.2 0.0 copy-start.2
  179.2 0.8 copy-done.2
  180.0 17.2 %combine.1 = bf16[8192,384]{1,0:T(8,128)(2,1)} custom-call(bf16[10240,384]{1,0:T(8,128)(2,1)S(1)} %copy-done, s32[64,128]{1,0:T(8,128)S(1)} %copy-done.1, f32[64,128]{1,0:T(8,128)S(1)} %copy-done.2), custom_call_target="tpu_custom_call" | custom-call | flops 20000000000 | bytes 15000000 | tf_op jit(solution)/shard_map/combine/pallas_call | solution.py:405
Async XLA Ops:
  26.3 149.7 %copy-start.1 = (s32[64,128]{1,0:T(8,128)S(1)}, s32[64,128]{1,0:T(8,128)}, u32[]{:S(2)}) copy-start(s32[64,128]{1,0:T(8,128)} %get-tuple-element.11.dest_sm) | copy-start | bytes 98308
  176.0 3.2 %copy-start = (bf16[10240,384]{1,0:T(8,128)(2,1)S(1)}, bf16[10240,384]{1,0:T(8,128)(2,1)}, u32[]{:S(2)}) copy-start(bf16[10240,384]{1,0:T(8,128)(2,1)} %get-tuple-element.10.back_hbm) | copy-start | bytes 23592964
  179.2 0.8 copy-start.2

commit v3 on v2

v3 whole, which is shorter than its diff:
```python
import functools

import jax
import jax.numpy as jnp
from jax import lax
from jax.experimental import pallas as pl
from jax.experimental.pallas import tpu as pltpu
from jax.sharding import PartitionSpec as P

EXPERT_AXES = ("ep_b", "ep_a")
LANES = 128
MESH_ID = pl.DeviceIdType.MESH
F32 = jnp.float32
BF16 = jnp.bfloat16


def iota(shape, dim):
    return lax.broadcasted_iota(jnp.int32, shape, dim)


def dot_nt(a, b):
    return lax.dot_general(a, b, (((1,), (1,)), ((), ())), preferred_element_type=F32)


def as_bf16(mask):
    return jnp.where(mask, 1.0, 0.0).astype(BF16)


def virtual_expert(ids, size_b, size_x):
    i_b, i_a = ids // (2 * size_x), ids % (2 * size_x)
    x, core = i_a // 2, i_a % 2
    return jnp.where(core == 0, x * size_b + i_b, size_b * size_x + i_b * size_x + x)


def dispatch_kernel(dims, ids_ref, order_ref, tok_hbm, send_hbm, dest_ref,
                    rid_s, both_s, kept_s, hi_s, lo_s, src_vm, src_sm, tok_vm, big, tmp, send, tok_sem, src_sem, out_sem):
    size_b, size_x, cap = dims
    rows, slot_rows = ids_ref.shape[0], src_vm.shape[0]
    parts = tok_hbm.shape[1] // LANES
    tok_copy = pltpu.make_async_copy(tok_hbm, tok_vm, tok_sem)
    tok_copy.start()
    num_experts = 2 * size_b * size_x
    per_expert = slot_rows // num_experts
    upper = as_bf16((iota((LANES, 2 * LANES), 0) <= iota((LANES, 2 * LANES), 1)) | (iota((LANES, 2 * LANES), 1) >= LANES))
    ids_t = ids_ref[...].astype(F32).T.astype(BF16)
    iota_rows = iota((rows, LANES), 0)
    iota_lane = iota((LANES, LANES), 0)
    iota_exp = iota((num_experts, LANES), 0)
    iota_slot = iota((slot_rows, LANES), 0)
    zero_count = jnp.zeros((num_experts, LANES), F32)

    def row(r):
        return pl.ds(r, 1)

    def cols(r):
        return pl.ds(pl.multiple_of(r * LANES, LANES), LANES)

    def each(body, unroll):
        lax.fori_loop(0, rows, lambda r, _: (body(r), 0)[1], 0, unroll=unroll)

    def ranked_id(r):
        o = order_ref[row(r), :]
        table = jnp.dot(ids_t, as_bf16(iota_rows == o // LANES), preferred_element_type=F32)
        rid_s[row(r), :] = jnp.sum(jnp.where(iota_lane == o % LANES, table, 0.0), axis=0, keepdims=True).astype(jnp.int32)

    def ranked_count(r):
        both_s[r] = jnp.dot(as_bf16(iota_exp == rid_s[row(r), :]), upper, preferred_element_type=F32)

    def position(mine, r, count):
        return jnp.sum(jnp.where(mine, both_s[r, :, :LANES] + count, 0.0), axis=0, keepdims=True)

    def ranked_kept(r, count):
        rank = position(iota_exp == rid_s[row(r), :], r, count)
        kept_s[row(r), :] = (rank <= float(cap)).astype(jnp.int32)
        return count + both_s[r, :, LANES:]

    def scatter_kept(r):
        o = order_ref[row(r), :]
        hi_s[:rows, cols(r)] = as_bf16((iota_rows == o // LANES) & (kept_s[row(r), :] > 0))
        lo_s[:, cols(r)] = as_bf16(iota_lane == o % LANES)

    each(ranked_id, 16)
    each(ranked_count, 16)
    lax.fori_loop(0, rows, ranked_kept, zero_count, unroll=8)
    each(scatter_kept, 8)
    kept_s[...] = dot_nt(hi_s[:rows, :], lo_s[...]).astype(jnp.int32)

    def expert_of(r):
        return virtual_expert(ids_ref[row(r), :], size_b, size_x)

    def mine_kept(r):
        return (iota_exp == expert_of(r)) & (kept_s[row(r), :] > 0)

    def token_count(r):
        both_s[r] = jnp.dot(as_bf16(mine_kept(r)), upper, preferred_element_type=F32)

    lane = iota((1, LANES), 1).astype(F32)

    def placed(r, count):
        place = position(mine_kept(r), r, count).astype(jnp.int32) - 1
        kept = kept_s[row(r), :] > 0
        expert = expert_of(r)
        dest_ref[row(r), :] = jnp.where(kept, expert * cap + place, num_experts * cap) * parts
        rid_s[row(r), :] = jnp.where(kept, expert * (per_expert * LANES) + place, slot_rows * LANES)
        return count + both_s[r, :, LANES:]

    def scatter_source(r):
        slot = rid_s[row(r), :]
        hit = jnp.where(iota_slot == slot // LANES, 1.0, 0.0)
        hi_s[:slot_rows, cols(r)] = (hit * lax.convert_element_type(r, F32)).astype(BF16)
        hi_s[slot_rows:, cols(r)] = (hit * lane).astype(BF16)
        lo_s[:, cols(r)] = as_bf16(iota_lane == slot % LANES)

    each(token_count, 16)
    lax.fori_loop(0, rows, placed, zero_count, unroll=8)
    each(scatter_source, 8)
    found = dot_nt(hi_s[...], lo_s[...])
    src_vm[...] = ((found[:slot_rows] * float(LANES) + found[slot_rows:]) * float(parts)).astype(jnp.int32)
    src_copy = pltpu.make_async_copy(src_vm, src_sm, src_sem)
    src_copy.start()

    tok_copy.wait()

    def widen(i, _):
        base = pl.multiple_of(i * 16, 16)
        for c in range(parts):
            big[pl.ds(base * parts + c, 16, stride=parts), :] = tok_vm[pl.ds(base, 16), c * LANES:(c + 1) * LANES].astype(F32)
        return 0

    lax.fori_loop(0, tok_vm.shape[0] // 16, widen, 0, unroll=8)
    src_copy.wait()

    def gather_rows(row_index, first, count):
        for u in range(count):
            tmp[pl.ds(u * parts, parts), :] = big[pl.ds(src_sm[row_index, u], parts), :]
        for u in range(0, count, 16):
            for c in range(parts):
                send[pl.ds(pl.multiple_of(first + u, 16), 16), c * LANES:(c + 1) * LANES] = (
                    tmp[pl.ds(u * parts + c, 16, stride=parts), :].astype(BF16))

    def out_copy(index):
        rows_of = pl.ds(pl.multiple_of(index * cap, cap), cap)
        return pltpu.make_async_copy(send.at[rows_of], send_hbm.at[rows_of], out_sem)

    def gather_block(index, _):
        def gather(g, _):
            gather_rows(index * per_expert + g, pl.multiple_of(index * cap + g * LANES, 16), LANES)
            return 0

        lax.fori_loop(0, cap // LANES, gather, 0)
        if cap % LANES:
            gather_rows(index * per_expert + cap // LANES, pl.multiple_of(index * cap + cap // LANES * LANES, 16), cap % LANES)
        out_copy(index).start()
        return 0

    lax.fori_loop(0, num_experts, gather_block, 0)
    lax.fori_loop(0, num_experts, lambda index, _: (out_copy(index).wait(), 0)[1], 0)


def dispatch(tok_rows, ids, order, dims):
    size_b, size_x, cap = dims
    num_experts = 2 * size_b * size_x
    slots, slot_rows = num_experts * cap, num_experts * pl.cdiv(cap, LANES)
    tok_dev, width = tok_rows.shape
    rows, parts = tok_dev // LANES, width // LANES
    vmem, hbm = pl.BlockSpec(memory_space=pltpu.VMEM), pl.BlockSpec(memory_space=pltpu.HBM)
    dma = pltpu.SemaphoreType.DMA
    return pl.pallas_call(
        functools.partial(dispatch_kernel, dims),
        name="dispatch",
        out_shape=(jax.ShapeDtypeStruct((slots, width), BF16), jax.ShapeDtypeStruct(ids.shape, jnp.int32)),
        in_specs=[vmem, vmem, hbm],
        out_specs=(hbm, vmem),
        scratch_shapes=[
            pltpu.VMEM((rows, LANES), jnp.int32),
            pltpu.VMEM((rows, num_experts, 2 * LANES), F32),
            pltpu.VMEM((rows, LANES), jnp.int32),
            pltpu.VMEM((2 * slot_rows, rows * LANES), BF16),
            pltpu.VMEM((LANES, rows * LANES), BF16),
            pltpu.VMEM((slot_rows, LANES), jnp.int32),
            pltpu.SMEM((slot_rows, LANES), jnp.int32),
            pltpu.VMEM((tok_dev, width), BF16),
            pltpu.VMEM((tok_dev * parts + 8, LANES), F32),
            pltpu.VMEM((LANES * parts + 8, LANES), F32),
            pltpu.VMEM((slots, width), BF16),
            dma, dma, dma,
        ],
        compiler_params=pltpu.CompilerParams(vmem_limit_bytes=60 << 20),
        cost_estimate=pl.CostEstimate(flops=20_000_000_000, bytes_accessed=15_000_000, transcendentals=0),
    )(ids, order, tok_rows)


def pick(table, t):
    value = jnp.int32(0)
    for i, entry in enumerate(table):
        if entry:
            value = value + jnp.where(t == i, entry, 0)
    return value


def experts_kernel(dims, ids_ref, wr_ref, keys_ref, tau_ref, tok_hbm, send, w1_hbm, w2_hbm, b1_hbm, b2_hbm,
                   back_hbm, gate_ref, stage, recv, w1, w2, b1, b2,
                   tok_sem, wout_sem, win_sem, out_sem, in_sem, ret_sem, back_sem):
    size_b, size_x, cap = dims
    n = size_x
    rows = ids_ref.shape[0]
    num_experts = 2 * size_b * size_x
    tok_dev, chunk = tok_hbm.shape[0], stage.shape[1]
    i_dp, i_b, i_a = lax.axis_index("dp"), lax.axis_index("ep_b"), lax.axis_index("ep_a")
    pos_x, core, pos_y = i_a // 2, lax.rem(i_a, 2), i_b
    pos = (1 - core) * pos_x + core * pos_y
    wpos = (1 - core) * pos_y + core * pos_x

    def sends_to(kind, k):
        return i_dp, (1 - kind) * pos_y + kind * k, 2 * ((1 - kind) * k + kind * pos_x) + kind

    def serves(k, c):
        return i_dp, core * k + (1 - core) * pos_y, 2 * (core * pos_x + (1 - core) * k) + c

    def shares(k):
        return i_dp, (1 - core) * k + core * pos_y, 2 * ((1 - core) * pos_x + core * k) + core

    def block(i):
        return pl.ds(pl.multiple_of(i * cap, cap), cap)

    def fetch(q):
        return pltpu.make_async_copy(tok_hbm.at[pl.ds(pl.multiple_of(q * chunk, chunk), chunk)], stage.at[lax.rem(q, 2)],
                                     tok_sem.at[lax.rem(q, 2)])

    def each_chunk(body):
        chunks = tok_dev // chunk

        def step(q, _):
            @pl.when(q + 1 < chunks)
            def _():
                fetch(q + 1).start()
            fetch(q).wait()
            body(q, lax.rem(q, 2))
            return 0

        lax.fori_loop(0, chunks, step, 0)

    fetch(0).start()
    held = ((w1_hbm, w1), (w2_hbm, w2), (b1_hbm, b1), (b2_hbm, b2))
    for i, (own, every) in enumerate(held):
        pltpu.make_async_copy(own, every.at[pl.ds(0, 1)], win_sem.at[i, 0]).start()

    barrier = pltpu.get_barrier_semaphore()
    for k in range(n):
        for c in range(2):
            for device in (sends_to(c, k), serves(k, c)):
                pl.semaphore_signal(barrier, inc=1, device_id=device, device_id_type=MESH_ID)
    for d in range(1, n):
        pl.semaphore_signal(barrier, inc=1, device_id=shares(lax.rem(wpos + d, n)), device_id_type=MESH_ID)
    pl.semaphore_wait(barrier, 5 * n - 1)

    def weight_copy(i, d):
        own, every = held[i]
        return pltpu.make_async_remote_copy(
            src_ref=own, dst_ref=every.at[pl.ds(d, 1)], send_sem=wout_sem.at[i, d], recv_sem=win_sem.at[i, d],
            device_id=shares(lax.rem(wpos - d + n, n)), device_id_type=MESH_ID)

    weight_order = [1, n - 1] + list(range(2, n - 1))
    for d in weight_order:
        for i in (2, 3, 0, 1):
            weight_copy(i, d).start()

    iota_exp = iota((num_experts, LANES), 0)

    near, far = [1, n - 1], list(range(2, n - 1))
    send_order = [(step, off, kind) for group in (near, far, [0]) for off in range(n) for step in group for kind in range(2)]

    def outgoing(t):
        step, off, kind = (pick([e[i] for e in send_order], t) for i in range(3))
        k = lax.rem((1 - kind) * pos_x + kind * pos_y + step, n)
        j = lax.rem((1 - kind) * pos_y + kind * pos_x + off, n)
        return step, kind, k, j

    def send_block(t):
        step, kind, k, j = outgoing(t)
        src = (kind * n + k) * n + j
        dst = (((1 - kind) * pos_x + kind * pos_y) * n + j) * 2 + core
        own = (step == 0) & (kind == core)

        @pl.when(own)
        def _():
            pltpu.make_async_copy(send.at[block(src)], recv.at[block(dst)], in_sem.at[dst]).start()

        @pl.when(jnp.logical_not(own))
        def _():
            pltpu.make_async_remote_copy(
                src_ref=send.at[block(src)], dst_ref=recv.at[block(dst)], send_sem=out_sem.at[src], recv_sem=in_sem.at[dst],
                device_id=sends_to(kind, k), device_id_type=MESH_ID).start()

    blocks = 2 * n * n
    lax.fori_loop(0, blocks, lambda t, _: (send_block(t), 0)[1], 0)

    keys = keys_ref[...].astype(F32)
    key_unit = keys / jnp.sqrt(jnp.sum(keys * keys, axis=1, keepdims=True))
    tau = tau_ref[0, 0]
    key_pad = jnp.concatenate([key_unit, jnp.zeros((LANES - num_experts, key_unit.shape[1]), F32)], axis=0)
    span = chunk // LANES

    def gate_rows(i, slot):
        r = jnp.dot(stage[slot], wr_ref[...], preferred_element_type=F32)
        unit = r / jnp.sqrt(jnp.sum(r * r, axis=1, keepdims=True))
        dots = lax.dot_general(unit, key_pad, (((1,), (1,)), ((), ())), preferred_element_type=F32,
                               precision=lax.Precision.HIGHEST)
        logits = dots.T[:num_experts] / tau
        p = jnp.exp(logits - jnp.max(logits, axis=0, keepdims=True))
        total = jnp.sum(p, axis=0, keepdims=True)
        for q in range(span):
            mine = iota_exp == ids_ref[pl.ds(i * span + q, 1), :]
            cols = slice(q * LANES, (q + 1) * LANES)
            gate_ref[pl.ds(i * span + q, 1), :] = jnp.sum(jnp.where(mine, p[:, cols], 0.0), axis=0, keepdims=True) / total[:, cols]

    each_chunk(gate_rows)

    serve_order = ([(0, off) for off in range(n // 2)] + [(step, off) for off in range(n) for step in near]
                   + [(0, off) for off in range(n // 2, n - 1)] + [(step, off) for step in far for off in range(n)] + [(0, n - 1)])
    first_use = [int(off not in [o for _, o in serve_order[:i]]) for i, (_, off) in enumerate(serve_order)]

    def incoming(t):
        step, off = (pick([e[i] for e in serve_order], t) for i in range(2))
        return lax.rem(pos - step + n, n), off, lax.rem(wpos + off, n)

    def result_ends(t, c):
        k, _, j = incoming(t)
        src, dst = (k * n + j) * 2 + c, (core * n + pos) * n + j
        return k, src, dst, (k == pos) & (core == c)

    def send_results(t):
        for c in range(2):
            k, src, dst, own = result_ends(t, c)

            @pl.when(own)
            def _():
                pltpu.make_async_copy(recv.at[block(src)], back_hbm.at[block(dst)], back_sem.at[dst]).start()

            @pl.when(jnp.logical_not(own))
            def _():
                pltpu.make_async_remote_copy(
                    src_ref=recv.at[block(src)], dst_ref=back_hbm.at[block(dst)], send_sem=ret_sem.at[src],
                    recv_sem=back_sem.at[dst], device_id=serves(k, c), device_id_type=MESH_ID).start()

    def serve(t, _):
        k, off, j = incoming(t)
        first = (k * n + j) * 2

        @pl.when(pick(first_use, t) == 1)
        def _():
            for i, (own, every) in enumerate(held):
                pltpu.make_async_copy(own, every.at[pl.ds(off, 1)], win_sem.at[i, off]).wait()

        for c in range(2):
            pltpu.make_async_copy(send.at[block(0)], recv.at[block(first + c)], in_sem.at[first + c]).wait()
        here = pl.ds(pl.multiple_of(first * cap, 2 * cap), 2 * cap)
        hidden = jnp.dot(recv[here, :], w1[off], preferred_element_type=F32) + b1[off].astype(F32)
        hidden = (0.5 * hidden * (1.0 + lax.erf(hidden * (0.5 ** 0.5)))).astype(BF16)
        y = jnp.dot(hidden, w2[off], preferred_element_type=F32) + b2[off].astype(F32)
        recv[here, :] = y.astype(BF16)

        @pl.when(t > 0)
        def _():
            send_results(t - 1)
        return 0

    lax.fori_loop(0, n * n, serve, 0)
    send_results(jnp.int32(n * n - 1))

    for d in range(1, n):
        for i in range(len(held)):
            weight_copy(i, d).wait_send()

    def drain(t, _):
        sent = pltpu.make_async_remote_copy(
            src_ref=send.at[block(t)], dst_ref=recv.at[block(t)], send_sem=out_sem.at[t], recv_sem=in_sem.at[t],
            device_id=(i_dp, i_b, i_a), device_id_type=MESH_ID)
        returned = pltpu.make_async_remote_copy(
            src_ref=recv.at[block(t)], dst_ref=back_hbm.at[block(t)], send_sem=ret_sem.at[t], recv_sem=back_sem.at[t],
            device_id=(i_dp, i_b, i_a), device_id_type=MESH_ID)
        kind, k = t // (n * n), lax.rem(t // n, n)

        @pl.when((kind != core) | (k != pos))
        def _():
            sent.wait_send()

        @pl.when((t // (2 * n) != pos) | (lax.rem(t, 2) != core))
        def _():
            returned.wait_send()

        returned.wait_recv()
        return 0

    lax.fori_loop(0, blocks, drain, 0)


def experts(tok_rows, ids, send_rows, w_route, expert_keys, temperature, w1, w2, b1, b2, dims):
    size_b, size_x, cap = dims
    n = size_x
    tok_dev, width = tok_rows.shape
    hidden = w1.shape[2]
    slots = send_rows.shape[0]
    vmem, smem, hbm = (pl.BlockSpec(memory_space=m) for m in (pltpu.VMEM, pltpu.SMEM, pltpu.HBM))
    dma = pltpu.SemaphoreType.DMA
    return pl.pallas_call(
        functools.partial(experts_kernel, dims),
        name="experts",
        out_shape=(jax.ShapeDtypeStruct((slots, width), BF16), jax.ShapeDtypeStruct(ids.shape, F32)),
        in_specs=[vmem] * 3 + [smem] + [hbm] * 6,
        out_specs=(hbm, vmem),
        scratch_shapes=[
            pltpu.VMEM((2, min(tok_dev, 512), width), BF16),
            pltpu.VMEM((slots, width), BF16),
            pltpu.VMEM((n, width, hidden), BF16),
            pltpu.VMEM((n, hidden, width), BF16),
            pltpu.VMEM((n, 1, hidden), BF16),
            pltpu.VMEM((n, 1, width), BF16),
            dma((2,)), dma((4, n)), dma((4, n)),
            dma((2 * n * n,)), dma((2 * n * n,)), dma((2 * n * n,)), dma((2 * n * n,)),
        ],
        compiler_params=pltpu.CompilerParams(collective_id=1, has_side_effects=True, vmem_limit_bytes=61 << 20),
        cost_estimate=pl.CostEstimate(flops=4 * slots * width * hidden, bytes_accessed=30_000_000, transcendentals=0),
    )(ids, w_route, expert_keys, temperature.reshape(1, 1), tok_rows, send_rows, w1, w2, b1, b2)


def combine_kernel(back_hbm, dest_hbm, gate_ref, out_ref, stage, big, tmp, dest_sm, sem, dest_sem):
    i = pl.program_id(0)
    slots, width = back_hbm.shape
    parts = width // LANES
    chunk = stage.shape[1]
    chunks = slots // chunk

    @pl.when(i == 0)
    def _():
        def fetch(q):
            return pltpu.make_async_copy(back_hbm.at[pl.ds(pl.multiple_of(q * chunk, chunk), chunk)], stage.at[lax.rem(q, 2)],
                                         sem.at[lax.rem(q, 2)])
        fetch(0).start()
        dest_copy = pltpu.make_async_copy(dest_hbm, dest_sm, dest_sem)
        dest_copy.start()
        big[pl.ds(slots * parts, 8), :] = jnp.zeros((8, LANES), F32)

        def widen_chunk(q, _):
            @pl.when(q + 1 < chunks)
            def _():
                fetch(q + 1).start()
            fetch(q).wait()

            def widen(u, _):
                base = pl.multiple_of(u * 16, 16)
                for c in range(parts):
                    big[pl.ds((q * chunk + base) * parts + c, 16, stride=parts), :] = (
                        stage[lax.rem(q, 2), pl.ds(base, 16), c * LANES:(c + 1) * LANES].astype(F32))
                return 0

            lax.fori_loop(0, chunk // 16, widen, 0, unroll=8)
            return 0

        lax.fori_loop(0, chunks, widen_chunk, 0)
        dest_copy.wait()

    def gather(g, _):
        row = i * (out_ref.shape[0] // LANES) + g
        for j in range(LANES):
            tmp[pl.ds(j * parts, parts), :] = big[pl.ds(dest_sm[row, j], parts), :]
        gate = jnp.broadcast_to(gate_ref[pl.ds(row, 1), :], (LANES, LANES)).T
        for j in range(0, LANES, 16):
            for c in range(parts):
                out_ref[pl.ds(pl.multiple_of(g * LANES + j, 16), 16), c * LANES:(c + 1) * LANES] = (
                    (gate[j:j + 16] * tmp[pl.ds(j * parts + c, 16, stride=parts), :]).astype(BF16))
        return 0

    lax.fori_loop(0, out_ref.shape[0] // LANES, gather, 0)


def combine(back_rows, dest, gate, tok_dev):
    slots, width = back_rows.shape
    parts = width // LANES
    block = 1024
    hbm = pl.BlockSpec(memory_space=pltpu.HBM)
    return pl.pallas_call(
        combine_kernel,
        name="combine",
        grid=(tok_dev // block,),
        out_shape=jax.ShapeDtypeStruct((tok_dev, width), BF16),
        in_specs=[hbm, hbm, pl.BlockSpec(memory_space=pltpu.VMEM)],
        out_specs=pl.BlockSpec((block, width), lambda i: (i, 0)),
        scratch_shapes=[
            pltpu.VMEM((2, 1280, width), BF16),
            pltpu.VMEM((slots * parts + 8, LANES), F32),
            pltpu.VMEM((LANES * parts + 8, LANES), F32),
            pltpu.SMEM(dest.shape, jnp.int32),
            pltpu.SemaphoreType.DMA((2,)),
            pltpu.SemaphoreType.DMA,
        ],
        compiler_params=pltpu.CompilerParams(vmem_limit_bytes=40 << 20, dimension_semantics=("arbitrary",)),
        cost_estimate=pl.CostEstimate(flops=20_000_000_000, bytes_accessed=15_000_000, transcendentals=0),
    )(back_rows, dest, gate)


def solution(mesh):
    size_b, size_x = mesh.shape["ep_b"], mesh.shape["ep_a"] // 2
    num_experts = 2 * size_b * size_x
    tok_spec = P(("dp",) + EXPERT_AXES)
    expert_spec = P(EXPERT_AXES)

    def device_step(tokens, expert_ids, route_order, w_route, expert_keys, temperature, w_in, b_in, w_out, b_out):
        tok_dev = tokens.shape[1]
        cap = (5 * tok_dev + 4 * num_experts - 1) // (4 * num_experts)
        dims = (size_b, size_x, cap)
        ids = expert_ids.reshape(tok_dev // LANES, LANES)
        send_rows, dest = dispatch(tokens[0], ids, route_order.reshape(ids.shape), dims)
        back_rows, gate = experts(tokens[0], ids, send_rows, w_route, expert_keys, temperature, w_in, w_out,
                                  b_in[:, None, :], b_out[:, None, :], dims)
        return combine(back_rows, dest, gate, tok_dev)[None]

    return jax.shard_map(
        device_step,
        mesh=mesh,
        in_specs=(tok_spec, tok_spec, tok_spec, P(), P(), P(), expert_spec, expert_spec, expert_spec, expert_spec),
        out_specs=tok_spec,
        check_vma=False,
    )
```

time: 198 us -> 191 us (0.965)
  Pallas kernels: 191 us -> 186 us
    pallas_call x1, Pallas kernels: 17.2 us -> 14.4 us  [combine(): pl.pallas_call(combine_kernel, name='combine', grid=(tok_dev // block,),...]
where the time goes in v3:
time: 191 us
  Pallas kernels  186 us (97%)
  local copies, waits for them, and re-layouts  3.99 us (2%)
    pallas_call x1, Pallas kernels, experts(): pl.pallas_call(functools.partial(experts_kernel, dims), name='experts', o...  148 us
    pallas_call x1, Pallas kernels, dispatch(): pl.pallas_call(functools.partial(dispatch_kernel, dims), name='dispatch',...  23.4 us
    pallas_call x1, Pallas kernels, combine(): pl.pallas_call(combine_kernel, name='combine', grid=(tok_dev // block,),...  14.4 us
    unnamed x6, local copies, waits for them, and re-layouts  3.99 us

profile of v3, /device:TPU:97, one launch (start us, length us, event | category | flops | bytes accessed | tf_op | source)
XLA Modules:
  0.0 190.8 jit_solution(12448905078592407879)
XLA Ops:
  0.7 23.4 %dispatch.1 = (bf16[10240,384]{1,0:T(8,128)(2,1)}, s32[64,128]{1,0:T(8,128)}) custom-call(s32[64,128]{1,0:T(8,128)} %bitcast.11, s32[64,128]{1,0:T(8,128)} %bitcast.10, bf16[8192,384]{1,0:T(8,128)(2,1)} %bitcast.8), custom_call_target="tpu_custom_call" | custom-call | flops 20000000000 | bytes 15000000 | tf_op jit(solution)/shard_map/dispatch/pallas_call | solution.py:168
  24.1 0.0 copy-start.1
  24.1 148.3 %experts.1 = (bf16[10240,384]{1,0:T(8,128)(2,1)}, f32[64,128]{1,0:T(8,128)}) custom-call(s32[64,128]{1,0:T(8,128)} %bitcast.12, bf16[384,256]{1,0:T(8,128)(2,1)} %wr_ref.1, bf16[32,256]{1,0:T(8,128)(2,1)} %keys_ref.1, f32[1,1]{1,0:T(1,128)} %bitcast.7.tau_ref, bf16[8192,384]{1,0:T(8,128)(2,1)} %bitcast.9, bf16[10240,384]{1,0:T(8,128)(2,1)} %get-tuple-element.9.send, ...), custom_call_target="tpu_custom_call" | custom-call | flops 24159191040 | bytes 30000000 | tf_op jit(solution)/shard_map/experts/pallas_call | solution.py:406
  172.4 0.0 copy-done.1
  172.4 0.0 copy-start
  172.4 3.2 %copy-done = bf16[10240,384]{1,0:T(8,128)(2,1)S(1)} copy-done((bf16[10240,384]{1,0:T(8,128)(2,1)S(1)}, bf16[10240,384]{1,0:T(8,128)(2,1)}, u32[]{:S(2)}) %copy-start) | copy-done | bytes 7864344
  175.6 0.0 copy-start.2
  175.6 0.8 copy-done.2
  176.4 14.4 %combine.1 = bf16[8192,384]{1,0:T(8,128)(2,1)} custom-call(bf16[10240,384]{1,0:T(8,128)(2,1)S(1)} %copy-done, s32[64,128]{1,0:T(8,128)S(1)} %copy-done.1, f32[64,128]{1,0:T(8,128)S(1)} %copy-done.2), custom_call_target="tpu_custom_call" | custom-call | flops 20000000000 | bytes 15000000 | tf_op jit(solution)/shard_map/combine/pallas_call | solution.py:482
Async XLA Ops:
  24.1 148.3 %copy-start.1 = (s32[64,128]{1,0:T(8,128)S(1)}, s32[64,128]{1,0:T(8,128)}, u32[]{:S(2)}) copy-start(s32[64,128]{1,0:T(8,128)} %get-tuple-element.11.dest_hbm) | copy-start | bytes 98308
  172.4 3.2 %copy-start = (bf16[10240,384]{1,0:T(8,128)(2,1)S(1)}, bf16[10240,384]{1,0:T(8,128)(2,1)}, u32[]{:S(2)}) copy-start(bf16[10240,384]{1,0:T(8,128)(2,1)} %get-tuple-element.10.back_hbm) | copy-start | bytes 23592964
  175.6 0.8 copy-start.2

commit v4 on v3

--- a/solution.py
+++ b/solution.py
@@ -260,15 +260,30 @@
             src_ref=own, dst_ref=every.at[pl.ds(d, 1)], send_sem=wout_sem.at[i, d], recv_sem=win_sem.at[i, d],
             device_id=shares(lax.rem(wpos - d + n, n)), device_id_type=MESH_ID)
 
-    weight_order = [1, n - 1] + list(range(2, n - 1))
-    for d in weight_order:
-        for i in (2, 3, 0, 1):
+    near, far = [1, n - 1], list(range(2, n - 1))
+    for d in near + far:
+        for i in (2, 3):
             weight_copy(i, d).start()
+    for first, d in enumerate(near):
+        for i in (first, 1 - first):
+            weight_copy(i, d).start()
+
+    def passed_on(i):
+        every = held[i][1]
+        d, to = near[i], (wpos - 1 + n, wpos + 1)[i]
+        return pltpu.make_async_remote_copy(
+            src_ref=every.at[pl.ds(d, 1)], dst_ref=every.at[pl.ds(2, 1)], send_sem=wout_sem.at[i, 2], recv_sem=win_sem.at[i, 2],
+            device_id=shares(lax.rem(to, n)), device_id_type=MESH_ID)
+
+    def weights_here(i, off):
+        own, every = held[i]
+        pltpu.make_async_copy(own, every.at[pl.ds(off, 1)], win_sem.at[i, off]).wait()
 
     iota_exp = iota((num_experts, LANES), 0)
 
-    near, far = [1, n - 1], list(range(2, n - 1))
-    send_order = [(step, off, kind) for group in (near, far, [0]) for off in range(n) for step in group for kind in range(2)]
+    soon = [0] + near
+    send_order = [(step, off, kind) for offs, group in ((soon, near), (soon, far), (soon, [0]), (far, near + far + [0]))
+                  for off in offs for step in group for kind in range(2)]
 
     def outgoing(t):
         step, off, kind = (pick([e[i] for e in send_order], t) for i in range(3))
@@ -293,7 +308,8 @@
                 device_id=sends_to(kind, k), device_id_type=MESH_ID).start()
 
     blocks = 2 * n * n
-    lax.fori_loop(0, blocks, lambda t, _: (send_block(t), 0)[1], 0)
+    early = 2 * len(near)
+    lax.fori_loop(0, early, lambda t, _: (send_block(t), 0)[1], 0)
 
     keys = keys_ref[...].astype(F32)
     key_unit = keys / jnp.sqrt(jnp.sum(keys * keys, axis=1, keepdims=True))
@@ -316,9 +332,15 @@
 
     each_chunk(gate_rows)
 
-    serve_order = ([(0, off) for off in range(n // 2)] + [(step, off) for off in range(n) for step in near]
-                   + [(0, off) for off in range(n // 2, n - 1)] + [(step, off) for step in far for off in range(n)] + [(0, n - 1)])
-    first_use = [int(off not in [o for _, o in serve_order[:i]]) for i, (_, off) in enumerate(serve_order)]
+    for i in range(2):
+        weights_here(i, near[i])
+        passed_on(i).start()
+    lax.fori_loop(early, blocks, lambda t, _: (send_block(t), 0)[1], 0)
+
+    serve_order = ([(0, off) for off in soon] + [(step, off) for off in soon for step in near]
+                   + [(step, off) for step in far for off in soon] + [(step, off) for off in far for step in near + far + [0]])
+    first_use = [[int(off not in [o for _, o in serve_order[:t]] and (i > 1 or off != near[i]))
+                  for t, (_, off) in enumerate(serve_order)] for i in range(len(held))]
 
     def incoming(t):
         step, off = (pick([e[i] for e in serve_order], t) for i in range(2))
@@ -347,10 +369,10 @@
         k, off, j = incoming(t)
         first = (k * n + j) * 2
 
-        @pl.when(pick(first_use, t) == 1)
-        def _():
-            for i, (own, every) in enumerate(held):
-                pltpu.make_async_copy(own, every.at[pl.ds(off, 1)], win_sem.at[i, off]).wait()
+        for i in range(len(held)):
+            @pl.when(pick(first_use[i], t) == 1)
+            def _():
+                weights_here(i, off)
 
         for c in range(2):
             pltpu.make_async_copy(send.at[block(0)], recv.at[block(first + c)], in_sem.at[first + c]).wait()
@@ -368,9 +390,9 @@
     lax.fori_loop(0, n * n, serve, 0)
     send_results(jnp.int32(n * n - 1))
 
-    for d in range(1, n):
+    for d in near + far:
         for i in range(len(held)):
-            weight_copy(i, d).wait_send()
+            (passed_on(i) if d == 2 and i < 2 else weight_copy(i, d)).wait_send()
 
     def drain(t, _):
         sent = pltpu.make_async_remote_copy(
@@ -424,7 +446,7 @@
     )(ids, w_route, expert_keys, temperature.reshape(1, 1), tok_rows, send_rows, w1, w2, b1, b2)
 
 
-def combine_kernel(back_hbm, dest_hbm, gate_ref, out_ref, stage, big, tmp, dest_sm, sem, dest_sem):
+def combine_kernel(back_hbm, dest_ref, gate_ref, out_ref, stage, big, tmp, dest_sm, sem, dest_sem):
     i = pl.program_id(0)
     slots, width = back_hbm.shape
     parts = width // LANES
@@ -437,7 +459,7 @@
             return pltpu.make_async_copy(back_hbm.at[pl.ds(pl.multiple_of(q * chunk, chunk), chunk)], stage.at[lax.rem(q, 2)],
                                          sem.at[lax.rem(q, 2)])
         fetch(0).start()
-        dest_copy = pltpu.make_async_copy(dest_hbm, dest_sm, dest_sem)
+        dest_copy = pltpu.make_async_copy(dest_ref, dest_sm, dest_sem)
         dest_copy.start()
         big[pl.ds(slots * parts, 8), :] = jnp.zeros((8, LANES), F32)
 
@@ -484,7 +506,7 @@
         name="combine",
         grid=(tok_dev // block,),
         out_shape=jax.ShapeDtypeStruct((tok_dev, width), BF16),
-        in_specs=[hbm, hbm, pl.BlockSpec(memory_space=pltpu.VMEM)],
+        in_specs=[hbm] + [pl.BlockSpec(memory_space=pltpu.VMEM)] * 2,
         out_specs=pl.BlockSpec((block, width), lambda i: (i, 0)),
         scratch_shapes=[
             pltpu.VMEM((2, 1280, width), BF16),

time: 191 us -> 178 us (0.932)
  Pallas kernels: 186 us -> 173 us
    pallas_call x1, Pallas kernels: 148 us -> 136 us  [experts(): pl.pallas_call(functools.partial(experts_kernel, dims), name='experts', o...]
where the time goes in v4:
time: 178 us
  Pallas kernels  173 us (97%)
  local copies, waits for them, and re-layouts  3.99 us (2%)
    pallas_call x1, Pallas kernels, experts(): pl.pallas_call(functools.partial(experts_kernel, dims), name='experts', o...  136 us
    pallas_call x1, Pallas kernels, dispatch(): pl.pallas_call(functools.partial(dispatch_kernel, dims), name='dispatch',...  23.4 us
    pallas_call x1, Pallas kernels, combine(): pl.pallas_call(combine_kernel, name='combine', grid=(tok_dev // block,),...  14.4 us
    unnamed x6, local copies, waits for them, and re-layouts  3.99 us

profile of v4, /device:TPU:97, one launch (start us, length us, event | category | flops | bytes accessed | tf_op | source)
XLA Modules:
  0.0 178.1 jit_solution(15652012764961908068)
XLA Ops:
  0.7 23.4 %dispatch.1 = (bf16[10240,384]{1,0:T(8,128)(2,1)}, s32[64,128]{1,0:T(8,128)}) custom-call(s32[64,128]{1,0:T(8,128)} %bitcast.11, s32[64,128]{1,0:T(8,128)} %bitcast.10, bf16[8192,384]{1,0:T(8,128)(2,1)} %bitcast.8), custom_call_target="tpu_custom_call" | custom-call | flops 20000000000 | bytes 15000000 | tf_op jit(solution)/shard_map/dispatch/pallas_call | solution.py:168
  24.1 0.0 copy-start.1
  24.1 135.5 %experts.1 = (bf16[10240,384]{1,0:T(8,128)(2,1)}, f32[64,128]{1,0:T(8,128)}) custom-call(s32[64,128]{1,0:T(8,128)} %bitcast.12, bf16[384,256]{1,0:T(8,128)(2,1)} %wr_ref.1, bf16[32,256]{1,0:T(8,128)(2,1)} %keys_ref.1, f32[1,1]{1,0:T(1,128)} %bitcast.7.tau_ref, bf16[8192,384]{1,0:T(8,128)(2,1)} %bitcast.9, bf16[10240,384]{1,0:T(8,128)(2,1)} %get-tuple-element.9.send, ...), custom_call_target="tpu_custom_call" | custom-call | flops 24159191040 | bytes 30000000 | tf_op jit(solution)/shard_map/experts/pallas_call | solution.py:428
  159.6 0.0 copy-done.1
  159.6 0.0 copy-start
  159.6 3.2 %copy-done = bf16[10240,384]{1,0:T(8,128)(2,1)S(1)} copy-done((bf16[10240,384]{1,0:T(8,128)(2,1)S(1)}, bf16[10240,384]{1,0:T(8,128)(2,1)}, u32[]{:S(2)}) %copy-start) | copy-done | bytes 7864344
  162.9 0.0 copy-start.2
  162.9 0.8 copy-done.2
  163.6 14.4 %combine.1 = bf16[8192,384]{1,0:T(8,128)(2,1)} custom-call(bf16[10240,384]{1,0:T(8,128)(2,1)S(1)} %copy-done, s32[64,128]{1,0:T(8,128)S(1)} %copy-done.1, f32[64,128]{1,0:T(8,128)S(1)} %copy-done.2), custom_call_target="tpu_custom_call" | custom-call | flops 20000000000 | bytes 15000000 | tf_op jit(solution)/shard_map/combine/pallas_call | solution.py:504
Async XLA Ops:
  24.1 135.5 %copy-start.1 = (s32[64,128]{1,0:T(8,128)S(1)}, s32[64,128]{1,0:T(8,128)}, u32[]{:S(2)}) copy-start(s32[64,128]{1,0:T(8,128)} %get-tuple-element.11.dest_ref) | copy-start | bytes 98308
  159.6 3.2 %copy-start = (bf16[10240,384]{1,0:T(8,128)(2,1)S(1)}, bf16[10240,384]{1,0:T(8,128)(2,1)}, u32[]{:S(2)}) copy-start(bf16[10240,384]{1,0:T(8,128)(2,1)} %get-tuple-element.10.back_hbm) | copy-start | bytes 23592964
  162.9 0.8 copy-start.2
